TPU v7x, 32 devices: a whole 2x2x4 slice. The times are simulated.
32 devices in a mesh: space: 8 (over y, x, core), member: 4 (over z).
Axes of the slice: x: 2, y: 2, z: 4, core: 2. Of those that a mesh axis runs over, the one named last changes fastest.
Arguments:
- latent: bfloat16 [16, 4096, 1024], P('member', 'space'), may hold values from -6 to 6
- w_in: bfloat16 [1024, 1024], replicated, may hold values from -0.1875 to 0.1875
- b_in: float32 [1024], replicated, may hold values from -3 to 3
- w_out: bfloat16 [1024, 96], replicated, may hold values from -0.1875 to 0.1875
- b_out: float32 [96], replicated, may hold values from -3 to 3
- target: float32 [4096, 96], P('space'), may hold values from -6 to 6
- area: float32 [4096], P('space'), may hold values from 0.5 to 40, as said below
- cell_of: int32 [4096], P('space'), may hold values from 0 to 255, as said below
Outputs:
- latent_grad: bfloat16 [16, 4096, 1024], P('member', 'space')
- scores: float32 [2], replicated
Inputs may be any that keep to these rules, and one draw needn't show every extreme that they name: `cell_of`: every node lies in one coarse cell; some cells hold no node. Positive area of each node.
All inputs are finite; a program needn't handle non-finite values.
Results may differ from a plain program's by a relative error of at most 0.03.
Values may be sent and summed in bfloat16 or wider, within the bound.
A program may use at most 64 MiB of HBM per device.

v0:
```python
import functools

import jax
import jax.numpy as jnp
from jax import lax
from jax.experimental import pallas as pl
from jax.experimental.pallas import tpu as pltpu
from jax.sharding import PartitionSpec as P

CELL_DEV = 32
COLS = 512
LANES = 128

epsilon = 1e-05
loss_scale = 4096.0
bf16, f32 = jnp.bfloat16, jnp.float32
MESH = pl.DeviceIdType.MESH


def dot_t(a, b):
    return lax.dot_general(a, b, (((1,), (1,)), ((), ())), preferred_element_type=f32)


def halves(value):
    high = value.astype(bf16).astype(f32)
    return high, value - high


def exchange(spaces, places, latent, w_in, b_in, w_out, b_out, target, area, cell_of,
             slope_out, turned_out, up_out, stats_out,
             lat_buf, w_buf, turned, slope_buf, act, psend, precv, p32, grad, gsend, grecv,
             hot, csum, csend, crecv, mrecv, dsend, drecv, lmem, lspace,
             load_sem, slope_sem, ps_sem, pr_sem, gs_sem, gr_sem, cs_sem, cr_sem,
             ms_sem, mr_sem, ds_sem, dr_sem, ls_sem, lr_sem, ts_sem, tr_sem):
    ms = lax.axis_index("space")
    mm = lax.axis_index("member")
    locals_, quarter, width = lat_buf.shape[1:]
    units = w_buf.shape[1]
    variables = w_out.shape[0]
    members = locals_ * places
    cells = CELL_DEV * spaces
    pair_scale = 1.0 / (members * (members - 1))

    def member_peer(o):
        return lax.rem(mm + o, places)

    def space_peer(o):
        return lax.rem(ms + o, spaces)

    def to_member(src, dst, ss, rs, o):
        peer = member_peer(o)
        return pltpu.make_async_remote_copy(
            src_ref=src(peer), dst_ref=dst.at[mm], send_sem=ss.at[peer], recv_sem=rs.at[mm],
            device_id={"member": peer}, device_id_type=MESH)

    def from_member(dst, ss, rs, o):
        peer = member_peer(o)
        return pltpu.make_async_remote_copy(
            src_ref=dst.at[peer], dst_ref=dst.at[peer], send_sem=ss.at[peer], recv_sem=rs.at[peer],
            device_id={"member": peer}, device_id_type=MESH)

    def to_space(src, dst, ss, rs, o):
        peer = space_peer(o)
        return pltpu.make_async_remote_copy(
            src_ref=src(peer), dst_ref=dst.at[ms], send_sem=ss.at[peer], recv_sem=rs.at[ms],
            device_id={"space": peer}, device_id_type=MESH)

    def from_space(dst, ss, rs, o):
        peer = space_peer(o)
        return pltpu.make_async_remote_copy(
            src_ref=dst.at[peer], dst_ref=dst.at[peer], send_sem=ss.at[peer], recv_sem=rs.at[peer],
            device_id={"space": peer}, device_id_type=MESH)

    def nodes_of(q):
        return pl.ds(pl.multiple_of(q * quarter, quarter), quarter)

    def load_chunk(i):
        q = lax.rem(mm + 1 + i, places)
        return pltpu.make_async_copy(latent.at[:, nodes_of(q), :], lat_buf.at[i], load_sem.at[i])

    def store_slope(i):
        q = lax.rem(mm + 1 + i, places)
        return pltpu.make_async_copy(slope_buf.at[i], slope_out.at[:, nodes_of(q), :], slope_sem.at[i])

    w_copy = pltpu.make_async_copy(w_in, w_buf, load_sem.at[places])
    w_copy.start()
    for i in range(places):
        load_chunk(i).start()
    barrier = pltpu.get_barrier_semaphore()
    for o in range(1, places):
        pl.semaphore_signal(barrier, inc=1, device_id={"member": member_peer(o)}, device_id_type=MESH)
    for o in range(1, spaces):
        pl.semaphore_signal(barrier, inc=1, device_id={"space": space_peer(o)}, device_id_type=MESH)

    match = lax.broadcasted_iota(jnp.int32, (cells, cell_of.shape[1]), 0) == cell_of[...]
    ones = jnp.where(match, 1.0, 0.0)
    hot[...] = ones.astype(bf16)
    counts = halves(jnp.sum(ones, axis=1, keepdims=True))
    areas = halves(jnp.sum(jnp.where(match, area[...], 0.0), axis=1, keepdims=True))
    whole = halves(jnp.sum(area[...], axis=1, keepdims=True))
    csum[...] = jnp.zeros_like(csum)
    t_high, t_low = halves(target[...])
    csum[locals_, :, :variables] = dot_t(hot[...], t_high.astype(bf16)) + dot_t(hot[...], t_low.astype(bf16))
    lane = lax.broadcasted_iota(jnp.int32, (cells, LANES), 1)
    meta = csum[locals_]
    for n, value in enumerate(counts + areas + whole):
        meta = jnp.where(lane == variables + n, value, meta)
    csum[locals_] = meta

    w_copy.wait()
    pl.semaphore_wait(barrier, places + spaces - 2)

    def forward(i, carry):
        q = lax.rem(mm + 1 + i, places)
        load_chunk(i).wait()

        def columns(n, inner):
            at = pl.ds(pl.multiple_of(n * COLS, COLS), COLS)
            rows = lat_buf[i].reshape(locals_ * quarter, width)
            x = jnp.dot(rows, w_buf[:, at], preferred_element_type=f32) + b_in[:, at]
            s = 0.5 * jnp.tanh(0.5 * x) + 0.5
            a = x * s
            act[:, at] = a.astype(bf16)
            slope_buf[i, :, :, at] = (s + a * (1.0 - s)).astype(bf16).reshape(locals_, quarter, COLS)
            return inner

        lax.fori_loop(0, units // COLS, columns, 0)
        store_slope(i).start()
        pred = dot_t(act[...], w_out[...]) + b_out[...]
        rounded = pred.astype(bf16)
        for j in range(locals_):
            block = rounded[j * quarter:(j + 1) * quarter]
            psend[q, j] = block.astype(f32).T.astype(bf16)
            csum[j, :, :variables] += jnp.dot(hot[:, nodes_of(q)], block, preferred_element_type=f32)
        return carry

    def forward_send(i, carry):
        forward(i, carry)
        to_member(lambda peer: psend.at[peer], precv, ps_sem, pr_sem, i + 1).start()
        return carry

    lax.fori_loop(0, places - 1, forward_send, 0)
    forward(places - 1, 0)

    for s in range(spaces):
        csend[s] = csum[:, s * CELL_DEV:(s + 1) * CELL_DEV, :].astype(bf16)
    for o in range(1, spaces):
        to_space(lambda peer: csend.at[peer], crecv, cs_sem, cr_sem, o).start()

    precv[mm] = psend[mm]
    truths = target[:, nodes_of(mm)]
    weight = area[:, nodes_of(mm)]
    for o in range(1, places):
        from_member(precv, ps_sem, pr_sem, o).wait_recv()

    def truth_step(m, total):
        p = precv[lax.div(m, locals_), lax.rem(m, locals_)].astype(f32)
        p32[m] = p
        d = p - truths
        sq = jnp.sum(d * d, axis=0, keepdims=True) * (1.0 / variables) + epsilon
        r = lax.rsqrt(sq)
        grad[m] = d * (r * (1.0 / members))
        return total + sq * r

    def pair_step(m, total):
        pm = p32[m]
        factors = []
        for r in range(1, members // 2 + 1):
            share = 0.5 if 2 * r == members else 1.0
            d = pm - p32[lax.rem(m + r, members)]
            sq = jnp.sum(d * d, axis=0, keepdims=True) * (1.0 / variables) + epsilon
            inv = lax.rsqrt(sq)
            total = total + share * (sq * inv)
            factors.append(inv * (share * pair_scale))
        mine = grad[m]
        for r in range(1, members // 2 + 1):
            k = lax.rem(m + r, members)
            part = (pm - p32[k]) * factors[r - 1]
            mine = mine - part
            grad[k] = grad[k] + part
        grad[m] = mine
        return total

    zero = jnp.zeros((1, quarter), f32)
    truth_total = lax.fori_loop(0, members, truth_step, zero)
    pair_total = lax.fori_loop(0, members // 2, pair_step, zero)

    crecv[ms] = csend[ms]
    for o in range(1, spaces):
        from_space(crecv, cs_sem, cr_sem, o).wait_recv()

    total = crecv[0].astype(f32)
    for s in range(1, spaces):
        total = total + crecv[s].astype(f32)
    meta = total[locals_]
    cell_count = meta[:, variables:variables + 1] + meta[:, variables + 1:variables + 2]
    cell_area = meta[:, variables + 2:variables + 3] + meta[:, variables + 3:variables + 4]
    all_area = meta[0:1, variables + 4:variables + 5] + meta[0:1, variables + 5:variables + 6]
    divisor = jnp.maximum(cell_count, 1.0)
    means = (total[:locals_] / divisor[None]).astype(bf16)
    mrecv[mm] = means
    for o in range(1, places):
        to_member(lambda peer: mrecv.at[mm], mrecv, ms_sem, mr_sem, o).start()

    pair_total = lax.fori_loop(members // 2, members, pair_step, pair_total)
    fine_loss = weight * (truth_total * (1.0 / members) - pair_total * pair_scale)
    scale = weight * (1.0 / variables)
    for o in list(range(1, places)) + [0]:
        peer = member_peer(o)
        for j in range(locals_):
            out = (grad[peer * locals_ + j] * scale).astype(bf16)
            if o:
                gsend[peer, j] = out
            else:
                grecv[peer, j] = out
        if o:
            to_member(lambda p: gsend.at[p], grecv, gs_sem, gr_sem, o).start()

    for o in range(1, places):
        from_member(mrecv, ms_sem, mr_sem, o).wait_recv()
    rows = locals_ * CELL_DEV
    own = means.astype(f32).reshape(rows, LANES)
    cell_lane = lax.broadcasted_iota(jnp.int32, (CELL_DEV, LANES), 1)
    cell_target = jnp.where(cell_lane < variables, meta / divisor, 0.0)

    def repeat(value):
        return jnp.concatenate([value] * locals_, axis=0)

    d = own - repeat(cell_target)
    sq = jnp.sum(d * d, axis=1, keepdims=True) * (1.0 / variables) + epsilon
    inv = lax.rsqrt(sq)
    coarse = d * (inv * (1.0 / members))
    coarse_dist = sq * inv * (1.0 / members)
    for o in range(places):
        peer = member_peer(o)
        for r in range(locals_):
            if o == 0 and r == 0:
                continue
            other = jnp.concatenate([mrecv[peer, (j + r) % locals_] for j in range(locals_)], axis=0)
            d = own - other.astype(f32)
            sq = jnp.sum(d * d, axis=1, keepdims=True) * (1.0 / variables) + epsilon
            inv = lax.rsqrt(sq)
            coarse = coarse - d * (inv * pair_scale)
            coarse_dist = coarse_dist - sq * inv * (0.5 * pair_scale)
    cell_weight = repeat(cell_area)
    per_cell = (coarse * (cell_weight * (1.0 / variables)) / repeat(divisor)).astype(bf16)
    dsend[...] = per_cell.reshape(locals_, CELL_DEV, LANES)
    for o in range(1, spaces):
        to_space(lambda peer: dsend, drecv, ds_sem, dr_sem, o).start()
    drecv[ms] = per_cell.reshape(locals_, CELL_DEV, LANES)
    coarse_loss = jnp.sum(cell_weight * coarse_dist, axis=0, keepdims=True)

    row = lax.broadcasted_iota(jnp.int32, (8, LANES), 0)
    lmem[mm] = jnp.where(row == 0, jnp.sum(fine_loss, axis=1, keepdims=True), coarse_loss)
    for o in range(1, places):
        to_member(lambda peer: lmem.at[mm], lmem, ls_sem, lr_sem, o).start()
    for o in range(1, places):
        from_member(lmem, ls_sem, lr_sem, o).wait_recv()
    loss = lmem[0]
    for m in range(1, places):
        loss = loss + lmem[m]
    lspace[ms] = loss
    for o in range(1, spaces):
        to_space(lambda peer: lspace.at[ms], lspace, ts_sem, tr_sem, o).start()

    def turn(n, carry):
        at = pl.ds(pl.multiple_of(n * COLS, COLS), COLS)
        turned[:, at] = w_buf[at, :].T
        return carry

    lax.fori_loop(0, width // COLS, turn, 0)
    turned_copy = pltpu.make_async_copy(turned, turned_out, load_sem.at[places])
    turned_copy.start()

    for o in range(1, places):
        from_member(grecv, gs_sem, gr_sem, o).wait_recv()
    for o in range(1, spaces):
        from_space(drecv, ds_sem, dr_sem, o).wait_recv()
    for j in range(locals_):
        piece = drecv[:, j].reshape(cells, LANES).astype(f32).T[:variables].astype(bf16)
        coarse_part = jnp.dot(piece, hot[...], preferred_element_type=f32)
        for q in range(places):
            at = slice(q * quarter, (q + 1) * quarter)
            both = grecv[q, j].astype(f32) + coarse_part[:, at]
            up_out[j, at, :] = both.T.astype(bf16)

    for o in range(1, spaces):
        from_space(lspace, ts_sem, tr_sem, o).wait_recv()
    loss = lspace[0]
    for s in range(1, spaces):
        loss = loss + lspace[s]
    stats_out[...] = jnp.where(row == 2, all_area, loss)

    for o in range(1, places):
        to_member(lambda peer: psend.at[peer], precv, ps_sem, pr_sem, o).wait_send()
        to_member(lambda peer: mrecv.at[mm], mrecv, ms_sem, mr_sem, o).wait_send()
        to_member(lambda peer: gsend.at[peer], grecv, gs_sem, gr_sem, o).wait_send()
        to_member(lambda peer: lmem.at[mm], lmem, ls_sem, lr_sem, o).wait_send()
    for o in range(1, spaces):
        to_space(lambda peer: csend.at[peer], crecv, cs_sem, cr_sem, o).wait_send()
        to_space(lambda peer: dsend, drecv, ds_sem, dr_sem, o).wait_send()
        to_space(lambda peer: lspace.at[ms], lspace, ts_sem, tr_sem, o).wait_send()
    for i in range(places):
        store_slope(i).wait()
    turned_copy.wait()


def backward(scaling, slope, up, w_out, turned, stats, latent_grad, scores, pg):
    locals_, quarter, units = slope.shape
    rows = locals_ * quarter
    all_area = stats[2:3, 0:1]
    factor = scaling / all_area
    lines = up[...].reshape(rows, up.shape[2])

    def hidden(n, carry):
        at = pl.ds(pl.multiple_of(n * COLS, COLS), COLS)
        h = jnp.dot(lines, w_out[:, at], preferred_element_type=f32)
        pg[:, at] = (h * slope[:, :, at].reshape(rows, COLS).astype(f32)).astype(bf16)
        return carry

    lax.fori_loop(0, units // COLS, hidden, 0)

    def outputs(n, carry):
        at = pl.ds(pl.multiple_of(n * COLS, COLS), COLS)
        g = jnp.dot(pg[...], turned[:, at], preferred_element_type=f32)
        latent_grad[:, :, at] = (g * factor).astype(bf16).reshape(locals_, quarter, COLS)
        return carry

    lax.fori_loop(0, turned.shape[1] // COLS, outputs, 0)
    both = stats[...] / all_area
    scores[0] = both[0, 0]
    scores[1] = both[1, 0]


def solution(mesh):
    spaces, places = mesh.shape["space"], mesh.shape["member"]

    def shards(latent, w_in, b_in, w_out, b_out, target, area, cell_of):
        locals_, nodes, width = latent.shape
        units, variables = w_out.shape
        quarter = nodes // places
        cells = CELL_DEV * spaces
        members = locals_ * places
        anywhere = pl.BlockSpec(memory_space=pl.ANY)
        inside = pl.BlockSpec(memory_space=pltpu.VMEM)
        by_member = [pltpu.SemaphoreType.DMA((places,))]
        by_space = [pltpu.SemaphoreType.DMA((spaces,))]
        slope, turned, up, stats = pl.pallas_call(
            functools.partial(exchange, spaces, places),
            out_shape=(
                jax.ShapeDtypeStruct((locals_, nodes, units), bf16),
                jax.ShapeDtypeStruct((units, width), bf16),
                jax.ShapeDtypeStruct((locals_, nodes, variables), bf16),
                jax.ShapeDtypeStruct((8, LANES), f32),
            ),
            in_specs=[anywhere, anywhere] + [inside] * 6,
            out_specs=(anywhere, anywhere, inside, inside),
            scratch_shapes=[
                pltpu.VMEM((places, locals_, quarter, width), bf16),
                pltpu.VMEM((width, units), bf16),
                pltpu.VMEM((units, width), bf16),
                pltpu.VMEM((places, locals_, quarter, units), bf16),
                pltpu.VMEM((locals_ * quarter, units), bf16),
                pltpu.VMEM((places, locals_, variables, quarter), bf16),
                pltpu.VMEM((places, locals_, variables, quarter), bf16),
                pltpu.VMEM((members, variables, quarter), f32),
                pltpu.VMEM((members, variables, quarter), f32),
                pltpu.VMEM((places, locals_, variables, quarter), bf16),
                pltpu.VMEM((places, locals_, variables, quarter), bf16),
                pltpu.VMEM((cells, nodes), bf16),
                pltpu.VMEM((locals_ + 1, cells, LANES), f32),
                pltpu.VMEM((spaces, locals_ + 1, CELL_DEV, LANES), bf16),
                pltpu.VMEM((spaces, locals_ + 1, CELL_DEV, LANES), bf16),
                pltpu.VMEM((places, locals_, CELL_DEV, LANES), bf16),
                pltpu.VMEM((locals_, CELL_DEV, LANES), bf16),
                pltpu.VMEM((spaces, locals_, CELL_DEV, LANES), bf16),
                pltpu.VMEM((places, 8, LANES), f32),
                pltpu.VMEM((spaces, 8, LANES), f32),
                pltpu.SemaphoreType.DMA((places + 1,)),
            ]
            + by_member * 5
            + by_space * 2
            + by_member * 2
            + by_space * 2
            + by_member * 2
            + by_space * 2,
            compiler_params=pltpu.CompilerParams(
                collective_id=0, has_side_effects=True, vmem_limit_bytes=62 * 2**20
            ),
            name="exchange",
        )(latent, w_in, b_in[None], w_out.T, b_out[None], target.T, area[None], cell_of[None])

        def whole(shape):
            return pl.BlockSpec(shape, lambda i: (0,) * len(shape))

        latent_grad, scores = pl.pallas_call(
            functools.partial(backward, loss_scale * (nodes * spaces)),
            grid=(places,),
            out_shape=(
                jax.ShapeDtypeStruct((locals_, nodes, width), bf16),
                jax.ShapeDtypeStruct((2,), f32),
            ),
            in_specs=[
                pl.BlockSpec((locals_, quarter, units), lambda i: (0, i, 0)),
                pl.BlockSpec((locals_, quarter, variables), lambda i: (0, i, 0)),
                whole((variables, units)),
                whole((units, width)),
                whole((8, LANES)),
            ],
            out_specs=(
                pl.BlockSpec((locals_, quarter, width), lambda i: (0, i, 0)),
                pl.BlockSpec(memory_space=pltpu.SMEM),
            ),
            scratch_shapes=[pltpu.VMEM((locals_ * quarter, units), bf16)],
            compiler_params=pltpu.CompilerParams(vmem_limit_bytes=62 * 2**20),
            name="backward",
        )(slope, up, w_out.T, turned, stats)
        return latent_grad, scores

    in_specs = (
        P("member", "space", None),
        P(),
        P(),
        P(),
        P(),
        P("space", None),
        P("space"),
        P("space"),
    )
    out_specs = (P("member", "space", None), P())
    return jax.shard_map(shards, mesh=mesh, in_specs=in_specs, out_specs=out_specs, check_vma=False)
```

profile of v0, /device:TPU:0, one launch (start us, length us, event | category | flops | bytes accessed | tf_op | source)
XLA Modules:
  0.0 53.0 jit_solution(14082049295334871543)
XLA Ops:
  0.6 40.9 %exchange.1 = (bf16[4,512,1024]{2,1,0:T(8,128)(2,1)}, bf16[1024,1024]{1,0:T(8,128)(2,1)}, bf16[4,512,96]{2,1,0:T(8,128)(2,1)}, f32[8,128]{1,0:T(8,128)}) custom-call(bf16[4,512,1024]{2,1,0:T(8,128)(2,1)} %latent.1, bf16[1024,1024]{1,0:T(8,128)(2,1)} %w_in.1, f32[1,1024]{1,0:T(1,128)} %bitcast.9, bf16[96,1024]{1,0:T(8,128)(2,1)} %bitcast.6, ...), custom_call_target="tpu_custom_call" | custom-call | tf_op jit(solution)/shard_map/exchange/pallas_call | solution.py:348
  41.5 11.5 %backward.1 = (bf16[4,512,1024]{2,1,0:T(8,128)(2,1)}, f32[2]{0:T(128)}) custom-call(bf16[4,512,1024]{2,1,0:T(8,128)(2,1)} %get-tuple-element.6.slope, bf16[4,512,96]{2,1,0:T(8,128)(2,1)} %get-tuple-element.7.up, bf16[96,1024]{1,0:T(8,128)(2,1)} %bitcast.7, bf16[1024,1024]{1,0:T(8,128)(2,1)} %get-tuple-element.8.turned, f32[8,128]{1,0:T(8,128)} %get-tuple-element.9.stats), custom_call_target="tpu_custom_call" | custom-call | tf_op jit(solution)/shard_map/backward/pallas_call | solution.py:396
where the time goes:
time: 53.2 us; the launch traced here: 53 us
  Pallas kernels  52.4 us (98%)
  between operations  0.64 us (1%)
    pallas_call x1, Pallas kernels, shards(): pl.pallas_call(functools.partial(exchange, spaces, places), out_shape=(ja...  40.9 us
    pallas_call x1, Pallas kernels, shards(): pl.pallas_call(functools.partial(backward, loss_scale * (nodes * spaces))...  11.5 us

commit v1 on v0

--- a/solution.py
+++ b/solution.py
@@ -17,6 +17,10 @@
 MESH = pl.DeviceIdType.MESH
 
 
+def in_hbm(value):
+    return pltpu.with_memory_space_constraint(value, pltpu.HBM)
+
+
 def dot_t(a, b):
     return lax.dot_general(a, b, (((1,), (1,)), ((), ())), preferred_element_type=f32)
 
@@ -26,11 +30,11 @@
     return high, value - high
 
 
-def exchange(spaces, places, latent, w_in, b_in, w_out, b_out, target, area, cell_of,
-             slope_out, turned_out, up_out, stats_out,
-             lat_buf, w_buf, turned, slope_buf, act, psend, precv, p32, grad, gsend, grecv,
-             hot, csum, csend, crecv, mrecv, dsend, drecv, lmem, lspace,
-             load_sem, slope_sem, ps_sem, pr_sem, gs_sem, gr_sem, cs_sem, cr_sem,
+def exchange(spaces, places, scaling, latent, w_in, b_in, w_out, b_out, target, area, cell_of,
+             early, pg_out, turned, stats_out,
+             lat_buf, w_buf, slope_buf, act, psend, precv, p32, grad, gsend, grecv,
+             hot, csum, csend, crecv, mrecv, dsend, drecv, pieces, up_buf, lmem, lspace,
+             load_sem, ps_sem, pr_sem, gs_sem, gr_sem, cs_sem, cr_sem,
              ms_sem, mr_sem, ds_sem, dr_sem, ls_sem, lr_sem, ts_sem, tr_sem):
     ms = lax.axis_index("space")
     mm = lax.axis_index("member")
@@ -77,10 +81,6 @@
     def load_chunk(i):
         q = lax.rem(mm + 1 + i, places)
         return pltpu.make_async_copy(latent.at[:, nodes_of(q), :], lat_buf.at[i], load_sem.at[i])
-
-    def store_slope(i):
-        q = lax.rem(mm + 1 + i, places)
-        return pltpu.make_async_copy(slope_buf.at[i], slope_out.at[:, nodes_of(q), :], slope_sem.at[i])
 
     w_copy = pltpu.make_async_copy(w_in, w_buf, load_sem.at[places])
     w_copy.start()
@@ -108,7 +108,6 @@
     csum[locals_] = meta
 
     w_copy.wait()
-    pl.semaphore_wait(barrier, places + spaces - 2)
 
     def forward(i, carry):
         q = lax.rem(mm + 1 + i, places)
@@ -121,11 +120,10 @@
             s = 0.5 * jnp.tanh(0.5 * x) + 0.5
             a = x * s
             act[:, at] = a.astype(bf16)
-            slope_buf[i, :, :, at] = (s + a * (1.0 - s)).astype(bf16).reshape(locals_, quarter, COLS)
+            slope_buf[i, :, at] = (s + a * (1.0 - s)).astype(bf16)
             return inner
 
         lax.fori_loop(0, units // COLS, columns, 0)
-        store_slope(i).start()
         pred = dot_t(act[...], w_out[...]) + b_out[...]
         rounded = pred.astype(bf16)
         for j in range(locals_):
@@ -136,6 +134,11 @@
 
     def forward_send(i, carry):
         forward(i, carry)
+
+        @pl.when(i == 0)
+        def _():
+            pl.semaphore_wait(barrier, places + spaces - 2)
+
         to_member(lambda peer: psend.at[peer], precv, ps_sem, pr_sem, i + 1).start()
         return carry
 
@@ -146,6 +149,13 @@
         csend[s] = csum[:, s * CELL_DEV:(s + 1) * CELL_DEV, :].astype(bf16)
     for o in range(1, spaces):
         to_space(lambda peer: csend.at[peer], crecv, cs_sem, cr_sem, o).start()
+
+    def turn(n, carry):
+        at = pl.ds(pl.multiple_of(n * COLS, COLS), COLS)
+        turned[:, at] = w_buf[at, :].T
+        return carry
+
+    lax.fori_loop(0, width // COLS, turn, 0)
 
     precv[mm] = psend[mm]
     truths = target[:, nodes_of(mm)]
@@ -205,16 +215,16 @@
     pair_total = lax.fori_loop(members // 2, members, pair_step, pair_total)
     fine_loss = weight * (truth_total * (1.0 / members) - pair_total * pair_scale)
     scale = weight * (1.0 / variables)
-    for o in list(range(1, places)) + [0]:
+
+    def send_grads(o):
         peer = member_peer(o)
         for j in range(locals_):
-            out = (grad[peer * locals_ + j] * scale).astype(bf16)
-            if o:
-                gsend[peer, j] = out
-            else:
-                grecv[peer, j] = out
-        if o:
-            to_member(lambda p: gsend.at[p], grecv, gs_sem, gr_sem, o).start()
+            gsend[peer, j] = (grad[peer * locals_ + j] * scale).astype(bf16)
+        to_member(lambda p: gsend.at[p], grecv, gs_sem, gr_sem, o).start()
+
+    send_grads(1)
+    for j in range(locals_):
+        grecv[mm, j] = (grad[mm * locals_ + j] * scale).astype(bf16)
 
     for o in range(1, places):
         from_member(mrecv, ms_sem, mr_sem, o).wait_recv()
@@ -254,6 +264,44 @@
     lmem[mm] = jnp.where(row == 0, jnp.sum(fine_loss, axis=1, keepdims=True), coarse_loss)
     for o in range(1, places):
         to_member(lambda peer: lmem.at[mm], lmem, ls_sem, lr_sem, o).start()
+    for o in range(2, places):
+        send_grads(o)
+
+    for o in range(1, spaces):
+        from_space(drecv, ds_sem, dr_sem, o).wait_recv()
+    for j in range(locals_):
+        pieces[j] = drecv[:, j].reshape(cells, LANES).astype(f32).T[:variables].astype(bf16)
+    factor = scaling / all_area
+
+    def upstream(i):
+        q = lax.rem(mm + 1 + i, places)
+        for j in range(locals_):
+            coarse_part = jnp.dot(pieces[j], hot[:, nodes_of(q)], preferred_element_type=f32)
+            both = grecv[q, j].astype(f32) + coarse_part
+            up_buf[j * quarter:(j + 1) * quarter, :] = both.T.astype(bf16)
+
+    def hidden_to(pg, i):
+        def hidden(n, carry):
+            at = pl.ds(pl.multiple_of(n * COLS, COLS), COLS)
+            h = jnp.dot(up_buf[...], w_out[:, at], preferred_element_type=f32)
+            pg[:, at] = (h * slope_buf[i, :, at].astype(f32)).astype(bf16)
+            return carry
+
+        lax.fori_loop(0, units // COLS, hidden, 0)
+
+    def finish(i):
+        upstream(i)
+        hidden_to(act, i)
+
+        def outputs(n, carry):
+            at = pl.ds(pl.multiple_of(n * COLS, COLS), COLS)
+            g = jnp.dot(act[...], turned[:, at], preferred_element_type=f32)
+            early[i - 1, :, :, at] = (g * factor).astype(bf16).reshape(locals_, quarter, COLS)
+            return carry
+
+        lax.fori_loop(0, width // COLS, outputs, 0)
+
+    finish(places - 1)
     for o in range(1, places):
         from_member(lmem, ls_sem, lr_sem, o).wait_recv()
     loss = lmem[0]
@@ -263,26 +311,16 @@
     for o in range(1, spaces):
         to_space(lambda peer: lspace.at[ms], lspace, ts_sem, tr_sem, o).start()
 
-    def turn(n, carry):
-        at = pl.ds(pl.multiple_of(n * COLS, COLS), COLS)
-        turned[:, at] = w_buf[at, :].T
+    def arrived(n, carry):
+        i = places - 2 - n
+        from_member(grecv, gs_sem, gr_sem, i + 1).wait_recv()
+        finish(i)
         return carry
 
-    lax.fori_loop(0, width // COLS, turn, 0)
-    turned_copy = pltpu.make_async_copy(turned, turned_out, load_sem.at[places])
-    turned_copy.start()
-
-    for o in range(1, places):
-        from_member(grecv, gs_sem, gr_sem, o).wait_recv()
-    for o in range(1, spaces):
-        from_space(drecv, ds_sem, dr_sem, o).wait_recv()
-    for j in range(locals_):
-        piece = drecv[:, j].reshape(cells, LANES).astype(f32).T[:variables].astype(bf16)
-        coarse_part = jnp.dot(piece, hot[...], preferred_element_type=f32)
-        for q in range(places):
-            at = slice(q * quarter, (q + 1) * quarter)
-            both = grecv[q, j].astype(f32) + coarse_part[:, at]
-            up_out[j, at, :] = both.T.astype(bf16)
+    lax.fori_loop(0, places - 2, arrived, 0)
+    from_member(grecv, gs_sem, gr_sem, 1).wait_recv()
+    upstream(0)
+    hidden_to(pg_out, 0)
 
     for o in range(1, spaces):
         from_space(lspace, ts_sem, tr_sem, o).wait_recv()
@@ -300,36 +338,44 @@
         to_space(lambda peer: csend.at[peer], crecv, cs_sem, cr_sem, o).wait_send()
         to_space(lambda peer: dsend, drecv, ds_sem, dr_sem, o).wait_send()
         to_space(lambda peer: lspace.at[ms], lspace, ts_sem, tr_sem, o).wait_send()
-    for i in range(places):
-        store_slope(i).wait()
-    turned_copy.wait()
-
-
-def backward(scaling, slope, up, w_out, turned, stats, latent_grad, scores, pg):
-    locals_, quarter, units = slope.shape
-    rows = locals_ * quarter
+
+
+def backward(places, scaling, early, pg, turned, stats, latent_grad, scores, last, store_sem):
+    locals_, quarter, width = last.shape
+    mm = lax.axis_index("member")
+
+    def nodes_of(i):
+        q = lax.rem(mm + 1 + i, places)
+        return pl.ds(pl.multiple_of(q * quarter, quarter), quarter)
+
+    def store(i):
+        return pltpu.make_async_copy(early.at[i - 1], latent_grad.at[:, nodes_of(i), :], store_sem.at[i - 1])
+
+    def store_last(n):
+        at = pl.ds(pl.multiple_of(n * COLS, COLS), COLS)
+        return pltpu.make_async_copy(
+            last.at[:, :, at], latent_grad.at[:, nodes_of(0), at], store_sem.at[places - 1 + n])
+
+    for i in range(1, places):
+        store(i).start()
     all_area = stats[2:3, 0:1]
     factor = scaling / all_area
-    lines = up[...].reshape(rows, up.shape[2])
-
-    def hidden(n, carry):
-        at = pl.ds(pl.multiple_of(n * COLS, COLS), COLS)
-        h = jnp.dot(lines, w_out[:, at], preferred_element_type=f32)
-        pg[:, at] = (h * slope[:, :, at].reshape(rows, COLS).astype(f32)).astype(bf16)
-        return carry
-
-    lax.fori_loop(0, units // COLS, hidden, 0)
 
     def outputs(n, carry):
         at = pl.ds(pl.multiple_of(n * COLS, COLS), COLS)
         g = jnp.dot(pg[...], turned[:, at], preferred_element_type=f32)
-        latent_grad[:, :, at] = (g * factor).astype(bf16).reshape(locals_, quarter, COLS)
+        last[:, :, at] = (g * factor).astype(bf16).reshape(locals_, quarter, COLS)
+        store_last(n).start()
         return carry
 
-    lax.fori_loop(0, turned.shape[1] // COLS, outputs, 0)
+    lax.fori_loop(0, width // COLS, outputs, 0)
     both = stats[...] / all_area
     scores[0] = both[0, 0]
     scores[1] = both[1, 0]
+    for i in range(1, places):
+        store(i).wait()
+    for n in range(width // COLS):
+        store_last(n).wait()
 
 
 def solution(mesh):
@@ -345,22 +391,23 @@
         inside = pl.BlockSpec(memory_space=pltpu.VMEM)
         by_member = [pltpu.SemaphoreType.DMA((places,))]
         by_space = [pltpu.SemaphoreType.DMA((spaces,))]
-        slope, turned, up, stats = pl.pallas_call(
-            functools.partial(exchange, spaces, places),
+        rows = locals_ * quarter
+        scaling = loss_scale * (nodes * spaces)
+        early, pg, turned, stats = pl.pallas_call(
+            functools.partial(exchange, spaces, places, scaling),
             out_shape=(
-                jax.ShapeDtypeStruct((locals_, nodes, units), bf16),
-                jax.ShapeDtypeStruct((units, width), bf16),
-                jax.ShapeDtypeStruct((locals_, nodes, variables), bf16),
-                jax.ShapeDtypeStruct((8, LANES), f32),
+                pltpu.VMEM((places - 1, locals_, quarter, width), bf16),
+                pltpu.VMEM((rows, units), bf16),
+                pltpu.VMEM((units, width), bf16),
+                pltpu.VMEM((8, LANES), f32),
             ),
             in_specs=[anywhere, anywhere] + [inside] * 6,
-            out_specs=(anywhere, anywhere, inside, inside),
+            out_specs=(inside, inside, inside, inside),
             scratch_shapes=[
                 pltpu.VMEM((places, locals_, quarter, width), bf16),
                 pltpu.VMEM((width, units), bf16),
-                pltpu.VMEM((units, width), bf16),
-                pltpu.VMEM((places, locals_, quarter, units), bf16),
-                pltpu.VMEM((locals_ * quarter, units), bf16),
+                pltpu.VMEM((places, rows, units), bf16),
+                pltpu.VMEM((rows, units), bf16),
                 pltpu.VMEM((places, locals_, variables, quarter), bf16),
                 pltpu.VMEM((places, locals_, variables, quarter), bf16),
                 pltpu.VMEM((members, variables, quarter), f32),
@@ -374,47 +421,39 @@
                 pltpu.VMEM((places, locals_, CELL_DEV, LANES), bf16),
                 pltpu.VMEM((locals_, CELL_DEV, LANES), bf16),
                 pltpu.VMEM((spaces, locals_, CELL_DEV, LANES), bf16),
+                pltpu.VMEM((locals_, variables, cells), bf16),
+                pltpu.VMEM((rows, variables), bf16),
                 pltpu.VMEM((places, 8, LANES), f32),
                 pltpu.VMEM((spaces, 8, LANES), f32),
                 pltpu.SemaphoreType.DMA((places + 1,)),
             ]
-            + by_member * 5
+            + by_member * 4
             + by_space * 2
             + by_member * 2
             + by_space * 2
             + by_member * 2
             + by_space * 2,
             compiler_params=pltpu.CompilerParams(
-                collective_id=0, has_side_effects=True, vmem_limit_bytes=62 * 2**20
+                collective_id=0, has_side_effects=True, vmem_limit_bytes=36 * 2**20
             ),
             name="exchange",
-        )(latent, w_in, b_in[None], w_out.T, b_out[None], target.T, area[None], cell_of[None])
-
-        def whole(shape):
-            return pl.BlockSpec(shape, lambda i: (0,) * len(shape))
+        )(in_hbm(latent), in_hbm(w_in), b_in[None], w_out.T, b_out[None], target.T, area[None], cell_of[None])
 
         latent_grad, scores = pl.pallas_call(
-            functools.partial(backward, loss_scale * (nodes * spaces)),
-            grid=(places,),
+            functools.partial(backward, places, scaling),
             out_shape=(
                 jax.ShapeDtypeStruct((locals_, nodes, width), bf16),
                 jax.ShapeDtypeStruct((2,), f32),
             ),
-            in_specs=[
-                pl.BlockSpec((locals_, quarter, units), lambda i: (0, i, 0)),
-                pl.BlockSpec((locals_, quarter, variables), lambda i: (0, i, 0)),
-                whole((variables, units)),
-                whole((units, width)),
-                whole((8, LANES)),
+            in_specs=[inside] * 4,
+            out_specs=(anywhere, pl.BlockSpec(memory_space=pltpu.SMEM)),
+            scratch_shapes=[
+                pltpu.VMEM((locals_, quarter, width), bf16),
+                pltpu.SemaphoreType.DMA((places - 1 + width // COLS,)),
             ],
-            out_specs=(
-                pl.BlockSpec((locals_, quarter, width), lambda i: (0, i, 0)),
-                pl.BlockSpec(memory_space=pltpu.SMEM),
-            ),
-            scratch_shapes=[pltpu.VMEM((locals_ * quarter, units), bf16)],
-            compiler_params=pltpu.CompilerParams(vmem_limit_bytes=62 * 2**20),
+            compiler_params=pltpu.CompilerParams(vmem_limit_bytes=16 * 2**20),
             name="backward",
-        )(slope, up, w_out.T, turned, stats)
+        )(early, pg, turned, stats)
         return latent_grad, scores
 
     in_specs = (

time: 53.2 us -> 46.5 us (0.87)
  Pallas kernels: 52.4 us -> 41 us
  local copies, waits for them, and re-layouts: 0 us -> 4.55 us
    pallas_call x2, Pallas kernels: 52.4 us -> 41 us  [the longest x1 38.2 us: shards(): pl.pallas_call(functools.partial(exchange, spaces, places, scaling), out_...]
    unnamed x0 -> x12, local copies, waits for them, and re-layouts: none -> 4.55 us
where the time goes in v1:
time: 46.5 us; the launch traced here: 46.2 us
  Pallas kernels  41 us (88%)
  local copies, waits for them, and re-layouts  4.55 us (10%)
  between operations  0.65 us (1%)
    pallas_call x1, Pallas kernels, shards(): pl.pallas_call(functools.partial(exchange, spaces, places, scaling), out_...  38.2 us
    unnamed x12, local copies, waits for them, and re-layouts  4.55 us
    pallas_call x1, Pallas kernels, shards(): pl.pallas_call(functools.partial(backward, places, scaling), out_shape=(j...  2.82 us

profile of v1, /device:TPU:0, one launch (start us, length us, event | category | flops | bytes accessed | tf_op | source)
XLA Modules:
  0.0 46.2 jit_solution(5480941249644647495)
XLA Ops:
  0.6 0.0 copy-start
  0.6 0.9 %copy-done = bf16[1024,96]{0,1:T(8,128)(2,1)S(1)} copy-done((bf16[1024,96]{0,1:T(8,128)(2,1)S(1)}, bf16[1024,96]{0,1:T(8,128)(2,1)}, u32[]{:S(2)}) %copy-start) | copy-done | bytes 196632
  1.6 0.0 copy-start.1
  1.6 0.9 %copy-done.1 = f32[512,96]{0,1:T(8,128)S(1)} copy-done((f32[512,96]{0,1:T(8,128)S(1)}, f32[512,96]{0,1:T(8,128)}, u32[]{:S(2)}) %copy-start.1) | copy-done | bytes 196632
  2.5 0.0 copy-start.2
  2.5 0.7 %copy-done.2 = f32[1024]{0:T(1024)S(1)} copy-done((f32[1024]{0:T(1024)S(1)}, f32[1024]{0:T(1024)}, u32[]{:S(2)}) %copy-start.2) | copy-done | bytes 4120
  3.2 0.0 copy-start.3
  3.2 0.7 %copy-done.3 = f32[512]{0:T(512)S(1)} copy-done((f32[512]{0:T(512)S(1)}, f32[512]{0:T(512)}, u32[]{:S(2)}) %copy-start.3) | copy-done | bytes 2072
  3.9 0.0 copy-start.4
  3.9 0.7 %copy-done.4 = s32[512]{0:T(512)S(1)} copy-done((s32[512]{0:T(512)S(1)}, s32[512]{0:T(512)}, u32[]{:S(2)}) %copy-start.4) | copy-done | bytes 2072
  4.5 0.0 copy-start.5
  4.5 0.7 %copy-done.5 = f32[96]{0:T(128)S(1)} copy-done((f32[96]{0:T(128)S(1)}, f32[96]{0:T(128)}, u32[]{:S(2)}) %copy-start.5) | copy-done | bytes 408
  5.2 38.2 %exchange.1 = (bf16[3,4,128,1024]{3,2,1,0:T(8,128)(2,1)S(1)}, bf16[512,1024]{1,0:T(8,128)(2,1)S(1)}, bf16[1024,1024]{1,0:T(8,128)(2,1)S(1)}, f32[8,128]{1,0:T(8,128)S(1)}) custom-call(bf16[4,512,1024]{2,1,0:T(8,128)(2,1)} %latent.1, bf16[1024,1024]{1,0:T(8,128)(2,1)} %w_in.1, f32[1,1024]{1,0:T(1,128)S(1)} %bitcast.8, bf16[96,1024]{1,0:T(8,128)(2,1)S(1)} %bitcast.6, ...), custom_call_target="tpu_custom_call" | custom-call | tf_op jit(solution)/shard_map/exchange/pallas_call | solution.py:396
  43.4 2.8 %backward.1 = (bf16[4,512,1024]{2,1,0:T(8,128)(2,1)}, f32[2]{0:T(128)}) custom-call(bf16[3,4,128,1024]{3,2,1,0:T(8,128)(2,1)S(1)} %get-tuple-element.6.early, bf16[512,1024]{1,0:T(8,128)(2,1)S(1)} %get-tuple-element.7.pg, bf16[1024,1024]{1,0:T(8,128)(2,1)S(1)} %get-tuple-element.8.turned, f32[8,128]{1,0:T(8,128)S(1)} %get-tuple-element.9.stats), custom_call_target="tpu_custom_call" | custom-call | tf_op jit(solution)/shard_map/backward/pallas_call | solution.py:442
Async XLA Ops:
  0.6 0.9 %copy-start = (bf16[1024,96]{0,1:T(8,128)(2,1)S(1)}, bf16[1024,96]{0,1:T(8,128)(2,1)}, u32[]{:S(2)}) copy-start(bf16[1024,96]{0,1:T(8,128)(2,1)} %param.11) | copy-start | bytes 589828
  1.6 0.9 %copy-start.1 = (f32[512,96]{0,1:T(8,128)S(1)}, f32[512,96]{0,1:T(8,128)}, u32[]{:S(2)}) copy-start(f32[512,96]{0,1:T(8,128)} %param.13) | copy-start | bytes 589828
  2.5 0.7 %copy-start.2 = (f32[1024]{0:T(1024)S(1)}, f32[1024]{0:T(1024)}, u32[]{:S(2)}) copy-start(f32[1024]{0:T(1024)} %param.10) | copy-start | bytes 12292
  3.2 0.7 %copy-start.3 = (f32[512]{0:T(512)S(1)}, f32[512]{0:T(512)}, u32[]{:S(2)}) copy-start(f32[512]{0:T(512)} %param.14) | copy-start | bytes 6148
  3.9 0.7 %copy-start.4 = (s32[512]{0:T(512)S(1)}, s32[512]{0:T(512)}, u32[]{:S(2)}) copy-start(s32[512]{0:T(512)} %param.15) | copy-start | bytes 6148
  4.5 0.7 %copy-start.5 = (f32[96]{0:T(128)S(1)}, f32[96]{0:T(128)}, u32[]{:S(2)}) copy-start(f32[96]{0:T(128)} %param.12) | copy-start | bytes 1156

commit v2 on v1

--- a/solution.py
+++ b/solution.py
@@ -30,11 +30,12 @@
     return high, value - high
 
 
-def exchange(spaces, places, scaling, latent, w_in, b_in, w_out, b_out, target, area, cell_of,
+def exchange(spaces, places, scaling, latent, w_in, b_in_far, w_out_far, b_out_far, target_far, area_far,
+             cell_of_far,
              early, pg_out, turned, stats_out,
-             lat_buf, w_buf, slope_buf, act, psend, precv, p32, grad, gsend, grecv,
-             hot, csum, csend, crecv, mrecv, dsend, drecv, pieces, up_buf, lmem, lspace,
-             load_sem, ps_sem, pr_sem, gs_sem, gr_sem, cs_sem, cr_sem,
+             b_in, w_out, b_out, target, area, cell_of, lat_buf, w_buf, slope_buf, act, psend, precv, p32, grad, gsend, grecv,
+             hot, turned_hot, csum, csend, crecv, mrecv, dsend, drecv, pieces, up_buf, lmem, lspace,
+             load_sem, small_sem, ps_sem, pr_sem, gs_sem, gr_sem, cs_sem, cr_sem,
              ms_sem, mr_sem, ds_sem, dr_sem, ls_sem, lr_sem, ts_sem, tr_sem):
     ms = lax.axis_index("space")
     mm = lax.axis_index("member")
@@ -83,8 +84,17 @@
         return pltpu.make_async_copy(latent.at[:, nodes_of(q), :], lat_buf.at[i], load_sem.at[i])
 
     w_copy = pltpu.make_async_copy(w_in, w_buf, load_sem.at[places])
+    small = [
+        pltpu.make_async_copy(src, dst, small_sem.at[n])
+        for n, (src, dst) in enumerate((
+            (cell_of_far, cell_of), (area_far, area), (target_far, target),
+            (b_in_far, b_in), (w_out_far, w_out), (b_out_far, b_out)))
+    ]
     w_copy.start()
-    for i in range(places):
+    load_chunk(0).start()
+    for copy in small:
+        copy.start()
+    for i in range(1, places):
         load_chunk(i).start()
     barrier = pltpu.get_barrier_semaphore()
     for o in range(1, places):
@@ -92,6 +102,8 @@
     for o in range(1, spaces):
         pl.semaphore_signal(barrier, inc=1, device_id={"space": space_peer(o)}, device_id_type=MESH)
 
+    for copy in small[:3]:
+        copy.wait()
     match = lax.broadcasted_iota(jnp.int32, (cells, cell_of.shape[1]), 0) == cell_of[...]
     ones = jnp.where(match, 1.0, 0.0)
     hot[...] = ones.astype(bf16)
@@ -107,23 +119,20 @@
         meta = jnp.where(lane == variables + n, value, meta)
     csum[locals_] = meta
 
+    for copy in small[3:]:
+        copy.wait()
     w_copy.wait()
 
     def forward(i, carry):
         q = lax.rem(mm + 1 + i, places)
         load_chunk(i).wait()
 
-        def columns(n, inner):
-            at = pl.ds(pl.multiple_of(n * COLS, COLS), COLS)
-            rows = lat_buf[i].reshape(locals_ * quarter, width)
-            x = jnp.dot(rows, w_buf[:, at], preferred_element_type=f32) + b_in[:, at]
-            s = 0.5 * jnp.tanh(0.5 * x) + 0.5
-            a = x * s
-            act[:, at] = a.astype(bf16)
-            slope_buf[i, :, at] = (s + a * (1.0 - s)).astype(bf16)
-            return inner
-
-        lax.fori_loop(0, units // COLS, columns, 0)
+        rows = lat_buf[i].reshape(locals_ * quarter, width)
+        x = jnp.dot(rows, w_buf[...], preferred_element_type=f32) + b_in[...]
+        s = 0.5 * jnp.tanh(0.5 * x) + 0.5
+        a = x * s
+        act[...] = a.astype(bf16)
+        slope_buf[i] = (s + a * (1.0 - s)).astype(bf16)
         pred = dot_t(act[...], w_out[...]) + b_out[...]
         rounded = pred.astype(bf16)
         for j in range(locals_):
@@ -156,6 +165,26 @@
         return carry
 
     lax.fori_loop(0, width // COLS, turn, 0)
+    for q in range(places):
+        at = slice(q * quarter, (q + 1) * quarter)
+        turned_hot[at, :] = hot[:, at].astype(f32).T.astype(bf16)
+
+    crecv[ms] = csend[ms]
+    for o in range(1, spaces):
+        from_space(crecv, cs_sem, cr_sem, o).wait_recv()
+
+    total = crecv[0].astype(f32)
+    for s in range(1, spaces):
+        total = total + crecv[s].astype(f32)
+    meta = total[locals_]
+    cell_count = meta[:, variables:variables + 1] + meta[:, variables + 1:variables + 2]
+    cell_area = meta[:, variables + 2:variables + 3] + meta[:, variables + 3:variables + 4]
+    all_area = meta[0:1, variables + 4:variables + 5] + meta[0:1, variables + 5:variables + 6]
+    divisor = jnp.maximum(cell_count, 1.0)
+    means = (total[:locals_] / divisor[None]).astype(bf16)
+    mrecv[mm] = means
+    for o in range(1, places):
+        to_member(lambda peer: mrecv.at[mm], mrecv, ms_sem, mr_sem, o).start()
 
     precv[mm] = psend[mm]
     truths = target[:, nodes_of(mm)]
@@ -193,26 +222,7 @@
 
     zero = jnp.zeros((1, quarter), f32)
     truth_total = lax.fori_loop(0, members, truth_step, zero)
-    pair_total = lax.fori_loop(0, members // 2, pair_step, zero)
-
-    crecv[ms] = csend[ms]
-    for o in range(1, spaces):
-        from_space(crecv, cs_sem, cr_sem, o).wait_recv()
-
-    total = crecv[0].astype(f32)
-    for s in range(1, spaces):
-        total = total + crecv[s].astype(f32)
-    meta = total[locals_]
-    cell_count = meta[:, variables:variables + 1] + meta[:, variables + 1:variables + 2]
-    cell_area = meta[:, variables + 2:variables + 3] + meta[:, variables + 3:variables + 4]
-    all_area = meta[0:1, variables + 4:variables + 5] + meta[0:1, variables + 5:variables + 6]
-    divisor = jnp.maximum(cell_count, 1.0)
-    means = (total[:locals_] / divisor[None]).astype(bf16)
-    mrecv[mm] = means
-    for o in range(1, places):
-        to_member(lambda peer: mrecv.at[mm], mrecv, ms_sem, mr_sem, o).start()
-
-    pair_total = lax.fori_loop(members // 2, members, pair_step, pair_total)
+    pair_total = lax.fori_loop(0, members, pair_step, zero)
     fine_loss = weight * (truth_total * (1.0 / members) - pair_total * pair_scale)
     scale = weight * (1.0 / variables)
 
@@ -269,37 +279,28 @@
 
     for o in range(1, spaces):
         from_space(drecv, ds_sem, dr_sem, o).wait_recv()
+    by_cell = [drecv[:, j].reshape(cells, LANES) for j in range(locals_)]
     for j in range(locals_):
-        pieces[j] = drecv[:, j].reshape(cells, LANES).astype(f32).T[:variables].astype(bf16)
+        pieces[:, j * LANES:(j + 1) * LANES] = by_cell[j]
     factor = scaling / all_area
 
     def upstream(i):
         q = lax.rem(mm + 1 + i, places)
+        coarse_part = jnp.dot(turned_hot[nodes_of(q), :], pieces[...], preferred_element_type=f32)
         for j in range(locals_):
-            coarse_part = jnp.dot(pieces[j], hot[:, nodes_of(q)], preferred_element_type=f32)
-            both = grecv[q, j].astype(f32) + coarse_part
-            up_buf[j * quarter:(j + 1) * quarter, :] = both.T.astype(bf16)
+            fine = grecv[q, j].astype(f32).T
+            up_buf[j * quarter:(j + 1) * quarter, :] = (
+                fine + coarse_part[:, j * LANES:j * LANES + variables]).astype(bf16)
 
     def hidden_to(pg, i):
-        def hidden(n, carry):
-            at = pl.ds(pl.multiple_of(n * COLS, COLS), COLS)
-            h = jnp.dot(up_buf[...], w_out[:, at], preferred_element_type=f32)
-            pg[:, at] = (h * slope_buf[i, :, at].astype(f32)).astype(bf16)
-            return carry
-
-        lax.fori_loop(0, units // COLS, hidden, 0)
+        h = jnp.dot(up_buf[...], w_out[...], preferred_element_type=f32)
+        pg[...] = (h * slope_buf[i].astype(f32)).astype(bf16)
 
     def finish(i):
         upstream(i)
         hidden_to(act, i)
-
-        def outputs(n, carry):
-            at = pl.ds(pl.multiple_of(n * COLS, COLS), COLS)
-            g = jnp.dot(act[...], turned[:, at], preferred_element_type=f32)
-            early[i - 1, :, :, at] = (g * factor).astype(bf16).reshape(locals_, quarter, COLS)
-            return carry
-
-        lax.fori_loop(0, width // COLS, outputs, 0)
+        g = jnp.dot(act[...], turned[...], preferred_element_type=f32)
+        early[i - 1] = (g * factor).astype(bf16).reshape(locals_, quarter, width)
 
     finish(places - 1)
     for o in range(1, places):
@@ -401,9 +402,15 @@
                 pltpu.VMEM((units, width), bf16),
                 pltpu.VMEM((8, LANES), f32),
             ),
-            in_specs=[anywhere, anywhere] + [inside] * 6,
+            in_specs=[anywhere] * 8,
             out_specs=(inside, inside, inside, inside),
             scratch_shapes=[
+                pltpu.VMEM((1, units), f32),
+                pltpu.VMEM((variables, units), bf16),
+                pltpu.VMEM((1, variables), f32),
+                pltpu.VMEM((variables, nodes), f32),
+                pltpu.VMEM((1, nodes), f32),
+                pltpu.VMEM((1, nodes), jnp.int32),
                 pltpu.VMEM((places, locals_, quarter, width), bf16),
                 pltpu.VMEM((width, units), bf16),
                 pltpu.VMEM((places, rows, units), bf16),
@@ -415,17 +422,19 @@
                 pltpu.VMEM((places, locals_, variables, quarter), bf16),
                 pltpu.VMEM((places, locals_, variables, quarter), bf16),
                 pltpu.VMEM((cells, nodes), bf16),
+                pltpu.VMEM((nodes, cells), bf16),
                 pltpu.VMEM((locals_ + 1, cells, LANES), f32),
                 pltpu.VMEM((spaces, locals_ + 1, CELL_DEV, LANES), bf16),
                 pltpu.VMEM((spaces, locals_ + 1, CELL_DEV, LANES), bf16),
                 pltpu.VMEM((places, locals_, CELL_DEV, LANES), bf16),
                 pltpu.VMEM((locals_, CELL_DEV, LANES), bf16),
                 pltpu.VMEM((spaces, locals_, CELL_DEV, LANES), bf16),
-                pltpu.VMEM((locals_, variables, cells), bf16),
+                pltpu.VMEM((cells, locals_ * LANES), bf16),
                 pltpu.VMEM((rows, variables), bf16),
                 pltpu.VMEM((places, 8, LANES), f32),
                 pltpu.VMEM((spaces, 8, LANES), f32),
                 pltpu.SemaphoreType.DMA((places + 1,)),
+                pltpu.SemaphoreType.DMA((6,)),
             ]
             + by_member * 4
             + by_space * 2
@@ -437,7 +446,7 @@
                 collective_id=0, has_side_effects=True, vmem_limit_bytes=36 * 2**20
             ),
             name="exchange",
-        )(in_hbm(latent), in_hbm(w_in), b_in[None], w_out.T, b_out[None], target.T, area[None], cell_of[None])
+        )(*map(in_hbm, (latent, w_in, b_in[None], w_out.T, b_out[None], target.T, area[None], cell_of[None])))
 
         latent_grad, scores = pl.pallas_call(
             functools.partial(backward, places, scaling),

time: 46.5 us -> 38.8 us (0.83)
  local copies, waits for them, and re-layouts: 4.55 us -> 0 us
  Pallas kernels: 41 us -> 38 us
    unnamed x12 -> x0, local copies, waits for them, and re-layouts: 4.55 us -> none
    pallas_call x1, Pallas kernels: 38.2 us -> 35.2 us  [shards(): pl.pallas_call(functools.partial(exchange, spaces, places, scaling), out_...]
where the time goes in v2:
time: 38.8 us; the launch traced here: 38.6 us
  Pallas kernels  38 us (98%)
  between operations  0.64 us (2%)
    pallas_call x1, Pallas kernels, shards(): pl.pallas_call(functools.partial(exchange, spaces, places, scaling), out_...  35.2 us
    pallas_call x1, Pallas kernels, shards(): pl.pallas_call(functools.partial(backward, places, scaling), out_shape=(j...  2.82 us

profile of v2, /device:TPU:0, one launch (start us, length us, event | category | flops | bytes accessed | tf_op | source)
XLA Modules:
  0.0 38.6 jit_solution(7086925220541957396)
XLA Ops:
  0.6 35.2 %exchange.1 = (bf16[3,4,128,1024]{3,2,1,0:T(8,128)(2,1)S(1)}, bf16[512,1024]{1,0:T(8,128)(2,1)S(1)}, bf16[1024,1024]{1,0:T(8,128)(2,1)S(1)}, f32[8,128]{1,0:T(8,128)S(1)}) custom-call(bf16[4,512,1024]{2,1,0:T(8,128)(2,1)} %latent.1, bf16[1024,1024]{1,0:T(8,128)(2,1)} %w_in.1, f32[1,1024]{1,0:T(1,128)} %bitcast.8, bf16[96,1024]{1,0:T(8,128)(2,1)} %bitcast.6, ...), custom_call_target="tpu_custom_call" | custom-call | tf_op jit(solution)/shard_map/exchange/pallas_call | solution.py:397
  35.8 2.8 %backward.1 = (bf16[4,512,1024]{2,1,0:T(8,128)(2,1)}, f32[2]{0:T(128)}) custom-call(bf16[3,4,128,1024]{3,2,1,0:T(8,128)(2,1)S(1)} %get-tuple-element.6.early, bf16[512,1024]{1,0:T(8,128)(2,1)S(1)} %get-tuple-element.7.pg, bf16[1024,1024]{1,0:T(8,128)(2,1)S(1)} %get-tuple-element.8.turned, f32[8,128]{1,0:T(8,128)S(1)} %get-tuple-element.9.stats), custom_call_target="tpu_custom_call" | custom-call | tf_op jit(solution)/shard_map/backward/pallas_call | solution.py:451

commit v3 on v2

v3 whole, which is shorter than its diff:
```python
import functools

import jax
import jax.numpy as jnp
from jax import lax
from jax.experimental import pallas as pl
from jax.experimental.pallas import tpu as pltpu
from jax.sharding import PartitionSpec as P

CELL_DEV = 32
COLS = 512
SLIM = 256
LANES = 128

epsilon = 1e-05
loss_scale = 4096.0
bf16, f32 = jnp.bfloat16, jnp.float32
MESH = pl.DeviceIdType.MESH


def in_hbm(value):
    return pltpu.with_memory_space_constraint(value, pltpu.HBM)


def dot_t(a, b):
    return lax.dot_general(a, b, (((1,), (1,)), ((), ())), preferred_element_type=f32)


def halves(value):
    high = value.astype(bf16).astype(f32)
    return high, value - high


def exchange(spaces, places, scaling, latent, w_in, b_in_far, w_out_far, b_out_far, target_far, area_far,
             cell_of_far,
             early, pg_out, turned, stats_out,
             b_in, w_out, b_out, target, area, cell_of, lat_buf, w_buf, slope_buf, act,
             psend, precv, p32, grad, gsend, grecv, hot, turned_hot, pcat, qsend, qrecv, csend, crecv,
             mrecv, dsend, drecv, up_buf, lmem, lspace,
             load_sem, small_sem, ps_sem, pr_sem, gs_sem, gr_sem, qs_sem, qr_sem, cs_sem, cr_sem,
             ms_sem, mr_sem, ds_sem, dr_sem, ls_sem, lr_sem, ts_sem, tr_sem):
    ms = lax.axis_index("space")
    mm = lax.axis_index("member")
    locals_, quarter, width = lat_buf.shape[1:]
    units = w_buf.shape[1]
    variables = target.shape[0]
    members = locals_ * places
    cells = CELL_DEV * spaces
    pair_scale = 1.0 / (members * (members - 1))

    def member_peer(o):
        return lax.rem(mm + o, places)

    def space_peer(o):
        return lax.rem(ms + o, spaces)

    def to_member(src, dst, ss, rs, o):
        return pltpu.make_async_remote_copy(
            src_ref=src, dst_ref=dst.at[mm], send_sem=ss, recv_sem=rs,
            device_id={"member": member_peer(o)}, device_id_type=MESH)

    def to_space(src, dst, ss, rs, o):
        return pltpu.make_async_remote_copy(
            src_ref=src, dst_ref=dst.at[ms], send_sem=ss, recv_sem=rs,
            device_id={"space": space_peer(o)}, device_id_type=MESH)

    def all_members(dst, ss, rs):
        part = dst.at[pl.ds(0, places - 1)]
        return pltpu.make_async_remote_copy(
            src_ref=part, dst_ref=part, send_sem=ss, recv_sem=rs,
            device_id={"member": member_peer(1)}, device_id_type=MESH)

    def all_spaces(dst, ss, rs):
        part = dst.at[pl.ds(0, spaces - 1)]
        return pltpu.make_async_remote_copy(
            src_ref=part, dst_ref=part, send_sem=ss, recv_sem=rs,
            device_id={"space": space_peer(1)}, device_id_type=MESH)

    def from_member(dst, ss, rs, o):
        peer = member_peer(o)
        return pltpu.make_async_remote_copy(
            src_ref=dst.at[peer], dst_ref=dst.at[peer], send_sem=ss, recv_sem=rs.at[peer],
            device_id={"member": peer}, device_id_type=MESH)

    def nodes_of(q):
        return pl.ds(pl.multiple_of(q * quarter, quarter), quarter)

    def load_chunk(i):
        q = lax.rem(mm + 1 + i, places)
        return pltpu.make_async_copy(latent.at[:, nodes_of(q), :], lat_buf.at[i], load_sem.at[i])

    w_copy = pltpu.make_async_copy(w_in, w_buf, load_sem.at[places])
    small = [
        pltpu.make_async_copy(src, dst, small_sem.at[n])
        for n, (src, dst) in enumerate((
            (cell_of_far, cell_of), (area_far, area), (target_far, target),
            (b_in_far, b_in), (w_out_far, w_out.at[pl.ds(0, variables)]), (b_out_far, b_out)))
    ]
    for copy in small[:3]:
        copy.start()
    w_copy.start()
    load_chunk(0).start()
    for copy in small[3:]:
        copy.start()
    for i in range(1, places):
        load_chunk(i).start()
    barrier = pltpu.get_barrier_semaphore()
    for o in range(1, places):
        pl.semaphore_signal(barrier, inc=1, device_id={"member": member_peer(o)}, device_id_type=MESH)
    for o in range(1, spaces):
        pl.semaphore_signal(barrier, inc=1, device_id={"space": space_peer(o)}, device_id_type=MESH)

    for copy in small[:3]:
        copy.wait()
    match = lax.broadcasted_iota(jnp.int32, (cells, cell_of.shape[1]), 0) == cell_of[...]
    ones = jnp.where(match, 1.0, 0.0)
    hot[...] = ones.astype(bf16)
    counts = halves(jnp.sum(ones, axis=1, keepdims=True))
    areas = halves(jnp.sum(jnp.where(match, area[...], 0.0), axis=1, keepdims=True))
    whole = halves(jnp.sum(area[...], axis=1, keepdims=True))
    spare = LANES - variables
    t_high, t_low = halves(target[...])
    sums = dot_t(hot[...], t_high.astype(bf16)) + dot_t(hot[...], t_low.astype(bf16))
    lane = lax.broadcasted_iota(jnp.int32, (cells, LANES), 1)
    meta = jnp.concatenate([sums, jnp.zeros((cells, spare), f32)], axis=1)
    for n, value in enumerate(counts + areas + whole):
        meta = jnp.where(lane == variables + n, value, meta)
    for s in range(spaces):
        qsend[s] = meta[s * CELL_DEV:(s + 1) * CELL_DEV].astype(bf16)
    w_out[variables:, :] = jnp.zeros((spare, units), bf16)

    for copy in small[3:]:
        copy.wait()
    w_copy.wait()

    def forward(i, carry):
        q = lax.rem(mm + 1 + i, places)
        load_chunk(i).wait()

        rows = lat_buf[i].reshape(locals_ * quarter, width)
        x = jnp.dot(rows, w_buf[...], preferred_element_type=f32) + b_in[...]
        act[...] = (x * (0.5 * jnp.tanh(0.5 * x) + 0.5)).astype(bf16)
        slope_buf[i] = x.astype(bf16)
        bias = jnp.concatenate([b_out[...], jnp.zeros((1, spare), f32)], axis=1)
        rounded = (dot_t(act[...], w_out[...]) + bias).astype(bf16)
        for j in range(locals_):
            block = rounded[j * quarter:(j + 1) * quarter]
            psend[q, j] = block.astype(f32).T[:variables].astype(bf16)
            pcat[nodes_of(q), j * LANES:(j + 1) * LANES] = block
        return carry

    def forward_send(i, carry):
        forward(i, carry)

        @pl.when(i == 0)
        def _():
            pl.semaphore_wait(barrier, places + spaces - 2)

        to_member(psend.at[member_peer(i + 1)], precv, ps_sem, pr_sem, i + 1).start()

        @pl.when(i == 0)
        def _():
            for o in range(1, spaces):
                to_space(qsend.at[space_peer(o)], qrecv, qs_sem, qr_sem, o).start()

        return carry

    lax.fori_loop(0, places - 1, forward_send, 0)
    forward(places - 1, 0)

    sums = jnp.dot(hot[...], pcat[...], preferred_element_type=f32).astype(bf16)
    for s in range(spaces):
        csend[s] = sums[s * CELL_DEV:(s + 1) * CELL_DEV]
    for o in range(1, spaces):
        to_space(csend.at[space_peer(o)], crecv, cs_sem, cr_sem, o).start()

    def turn(n, carry):
        at = pl.ds(pl.multiple_of(n * COLS, COLS), COLS)
        turned[:, at] = w_buf[at, :].T
        return carry

    lax.fori_loop(0, width // COLS, turn, 0)
    for q in range(places):
        at = slice(q * quarter, (q + 1) * quarter)
        turned_hot[at, :] = hot[:, at].astype(f32).T.astype(bf16)

    qrecv[ms] = qsend[ms]
    all_spaces(qrecv, qs_sem, qr_sem).wait_recv()
    meta = qrecv[0].astype(f32)
    for s in range(1, spaces):
        meta = meta + qrecv[s].astype(f32)
    cell_count = meta[:, variables:variables + 1] + meta[:, variables + 1:variables + 2]
    cell_area = meta[:, variables + 2:variables + 3] + meta[:, variables + 3:variables + 4]
    all_area = meta[0:1, variables + 4:variables + 5] + meta[0:1, variables + 5:variables + 6]
    divisor = jnp.maximum(cell_count, 1.0)
    cell_lane = lax.broadcasted_iota(jnp.int32, (CELL_DEV, LANES), 1)
    facts = jnp.where(cell_lane < variables, meta / divisor, jnp.where(cell_lane == variables, divisor, cell_area))
    facts = jnp.concatenate([facts] * locals_, axis=0).T
    cell_target = facts[:variables]
    lane_divisor = facts[variables:variables + 1]
    cell_weight = facts[variables + 1:variables + 2]

    def slopes(n, carry):
        i, at = lax.div(n, units // SLIM), pl.ds(pl.multiple_of(lax.rem(n, units // SLIM) * SLIM, SLIM), SLIM)
        x = slope_buf[i, :, at].astype(f32)
        s = 0.5 * jnp.tanh(0.5 * x) + 0.5
        slope_buf[i, :, at] = (s + x * s * (1.0 - s)).astype(bf16)
        return carry

    half = places // 2 * (units // SLIM)
    lax.fori_loop(0, half, slopes, 0)

    crecv[ms] = csend[ms]
    all_spaces(crecv, cs_sem, cr_sem).wait_recv()
    total = crecv[0].astype(f32)
    for s in range(1, spaces):
        total = total + crecv[s].astype(f32)
    means = (total / divisor).astype(bf16).astype(f32)
    own = jnp.concatenate([means[:, j * LANES:(j + 1) * LANES] for j in range(locals_)], axis=0).T[:variables]
    mrecv[mm] = own.astype(bf16)
    for o in range(1, places):
        to_member(mrecv.at[mm], mrecv, ms_sem, mr_sem, o).start()

    precv[mm] = psend[mm]
    truths = target[:, nodes_of(mm)]
    weight = area[:, nodes_of(mm)]
    all_members(precv, ps_sem, pr_sem).wait_recv()

    def truth_step(m, total):
        p = precv[lax.div(m, locals_), lax.rem(m, locals_)].astype(f32)
        p32[m] = p
        d = p - truths
        sq = jnp.sum(d * d, axis=0, keepdims=True) * (1.0 / variables) + epsilon
        r = lax.rsqrt(sq)
        grad[m] = d * (r * (1.0 / members))
        return total + sq * r

    def pair_step(m, total):
        pm = p32[m]
        factors = []
        for r in range(1, members // 2 + 1):
            share = 0.5 if 2 * r == members else 1.0
            d = pm - p32[lax.rem(m + r, members)]
            sq = jnp.sum(d * d, axis=0, keepdims=True) * (1.0 / variables) + epsilon
            inv = lax.rsqrt(sq)
            total = total + share * (sq * inv)
            factors.append(inv * (share * pair_scale))
        mine = grad[m]
        for r in range(1, members // 2 + 1):
            k = lax.rem(m + r, members)
            part = (pm - p32[k]) * factors[r - 1]
            mine = mine - part
            grad[k] = grad[k] + part
        grad[m] = mine
        return total

    zero = jnp.zeros((1, quarter), f32)
    truth_total = lax.fori_loop(0, members, truth_step, zero)
    pair_total = lax.fori_loop(0, members, pair_step, zero)
    fine_loss = weight * (truth_total * (1.0 / members) - pair_total * pair_scale)
    scale = weight * (1.0 / variables)

    def send_grads(o):
        peer = member_peer(o)
        for j in range(locals_):
            gsend[peer, j] = (grad[peer * locals_ + j] * scale).astype(bf16)
        to_member(gsend.at[peer], grecv, gs_sem, gr_sem.at[mm], o).start()

    send_grads(1)
    for j in range(locals_):
        grecv[mm, j] = (grad[mm * locals_ + j] * scale).astype(bf16)

    lax.fori_loop(half, places * (units // SLIM), slopes, 0)

    all_members(mrecv, ms_sem, mr_sem).wait_recv()
    d = own - cell_target
    sq = jnp.sum(d * d, axis=0, keepdims=True) * (1.0 / variables) + epsilon
    inv = lax.rsqrt(sq)
    coarse = d * (inv * (1.0 / members))
    coarse_dist = sq * inv * (1.0 / members)
    for o in range(places):
        theirs = mrecv[member_peer(o)].astype(f32)
        for r in range(locals_):
            if o == 0 and r == 0:
                continue
            d = own - (pltpu.roll(theirs, r * CELL_DEV, 1) if r else theirs)
            sq = jnp.sum(d * d, axis=0, keepdims=True) * (1.0 / variables) + epsilon
            inv = lax.rsqrt(sq)
            coarse = coarse - d * (inv * pair_scale)
            coarse_dist = coarse_dist - sq * inv * (0.5 * pair_scale)
    per_cell = coarse * (cell_weight * (1.0 / variables)) / lane_divisor
    per_cell = jnp.concatenate([per_cell, jnp.zeros((spare, locals_ * CELL_DEV), f32)], axis=0).T.astype(bf16)
    for j in range(locals_):
        dsend[:, j * LANES:(j + 1) * LANES] = per_cell[j * CELL_DEV:(j + 1) * CELL_DEV]
    for o in range(1, spaces):
        to_space(dsend, drecv, ds_sem, dr_sem, o).start()
    drecv[ms] = dsend[...]
    coarse_loss = jnp.sum(cell_weight * coarse_dist, axis=1, keepdims=True)

    row = lax.broadcasted_iota(jnp.int32, (8, LANES), 0)
    lmem[mm] = jnp.where(row == 0, jnp.sum(fine_loss, axis=1, keepdims=True), coarse_loss)
    for o in range(1, places):
        to_member(lmem.at[mm], lmem, ls_sem, lr_sem, o).start()
    for o in range(2, places):
        send_grads(o)

    all_spaces(drecv, ds_sem, dr_sem).wait_recv()
    factor = scaling / all_area

    def upstream(i):
        q = lax.rem(mm + 1 + i, places)
        pieces = drecv[...].reshape(cells, locals_ * LANES)
        coarse_part = jnp.dot(turned_hot[nodes_of(q), :], pieces, preferred_element_type=f32)
        blank = jnp.zeros((spare, quarter), f32)
        for j in range(locals_):
            fine = jnp.concatenate([grecv[q, j].astype(f32), blank], axis=0).T
            up_buf[j * quarter:(j + 1) * quarter, :] = (
                fine + coarse_part[:, j * LANES:(j + 1) * LANES]).astype(bf16)

    def hidden_to(pg, i):
        h = jnp.dot(up_buf[...], w_out[...], preferred_element_type=f32)
        pg[...] = (h * slope_buf[i].astype(f32)).astype(bf16)

    def finish(i):
        upstream(i)
        hidden_to(act, i)
        g = jnp.dot(act[...], turned[...], preferred_element_type=f32)
        early[i - 1] = (g * factor).astype(bf16).reshape(locals_, quarter, width)

    finish(places - 1)
    all_members(lmem, ls_sem, lr_sem).wait_recv()
    loss = lmem[0]
    for m in range(1, places):
        loss = loss + lmem[m]
    lspace[ms] = loss
    for o in range(1, spaces):
        to_space(lspace.at[ms], lspace, ts_sem, tr_sem, o).start()

    def arrived(n, carry):
        i = places - 2 - n
        from_member(grecv, gs_sem, gr_sem, i + 1).wait_recv()
        finish(i)
        return carry

    lax.fori_loop(0, places - 2, arrived, 0)
    from_member(grecv, gs_sem, gr_sem, 1).wait_recv()
    upstream(0)
    hidden_to(pg_out, 0)

    all_spaces(lspace, ts_sem, tr_sem).wait_recv()
    loss = lspace[0]
    for s in range(1, spaces):
        loss = loss + lspace[s]
    stats_out[...] = jnp.where(row == 2, all_area, loss)

    all_members(psend, ps_sem, pr_sem).wait_send()
    all_members(mrecv, ms_sem, mr_sem).wait_send()
    all_members(gsend, gs_sem, gr_sem.at[mm]).wait_send()
    all_members(lmem, ls_sem, lr_sem).wait_send()
    all_spaces(qsend, qs_sem, qr_sem).wait_send()
    all_spaces(csend, cs_sem, cr_sem).wait_send()
    all_spaces(drecv, ds_sem, dr_sem).wait_send()
    all_spaces(lspace, ts_sem, tr_sem).wait_send()


def backward(places, scaling, early, pg, turned, stats, latent_grad, scores_out, last, scores, store_sem):
    locals_, quarter, width = last.shape
    mm = lax.axis_index("member")

    def nodes_of(i):
        q = lax.rem(mm + 1 + i, places)
        return pl.ds(pl.multiple_of(q * quarter, quarter), quarter)

    def store(i):
        return pltpu.make_async_copy(early.at[i - 1], latent_grad.at[:, nodes_of(i), :], store_sem.at[i - 1])

    def store_last(n):
        at = pl.ds(pl.multiple_of(n * COLS, COLS), COLS)
        return pltpu.make_async_copy(
            last.at[:, :, at], latent_grad.at[:, nodes_of(0), at], store_sem.at[places - 1 + n])

    for i in range(1, places):
        store(i).start()
    all_area = stats[2:3, 0:1]
    factor = scaling / all_area
    both = stats[...] / all_area
    scores[0] = both[0, 0]
    scores[1] = both[1, 0]
    score_copy = pltpu.make_async_copy(scores, scores_out, store_sem.at[places - 1 + width // COLS])
    score_copy.start()

    def outputs(n, carry):
        at = pl.ds(pl.multiple_of(n * COLS, COLS), COLS)
        g = jnp.dot(pg[...], turned[:, at], preferred_element_type=f32)
        last[:, :, at] = (g * factor).astype(bf16).reshape(locals_, quarter, COLS)
        store_last(n).start()
        return carry

    lax.fori_loop(0, width // COLS, outputs, 0)
    score_copy.wait()
    for i in range(1, places):
        store(i).wait()
    for n in range(width // COLS):
        store_last(n).wait()


def solution(mesh):
    spaces, places = mesh.shape["space"], mesh.shape["member"]

    def shards(latent, w_in, b_in, w_out, b_out, target, area, cell_of):
        locals_, nodes, width = latent.shape
        units, variables = w_out.shape
        quarter = nodes // places
        cells = CELL_DEV * spaces
        members = locals_ * places
        anywhere = pl.BlockSpec(memory_space=pl.ANY)
        inside = pl.BlockSpec(memory_space=pltpu.VMEM)
        single = pltpu.SemaphoreType.DMA
        rows = locals_ * quarter
        scaling = loss_scale * (nodes * spaces)
        early, pg, turned, stats = pl.pallas_call(
            functools.partial(exchange, spaces, places, scaling),
            out_shape=(
                pltpu.VMEM((places - 1, locals_, quarter, width), bf16),
                pltpu.VMEM((rows, units), bf16),
                pltpu.VMEM((units, width), bf16),
                pltpu.VMEM((8, LANES), f32),
            ),
            in_specs=[anywhere] * 8,
            out_specs=(inside, inside, inside, inside),
            scratch_shapes=[
                pltpu.VMEM((1, units), f32),
                pltpu.VMEM((LANES, units), bf16),
                pltpu.VMEM((1, variables), f32),
                pltpu.VMEM((variables, nodes), f32),
                pltpu.VMEM((1, nodes), f32),
                pltpu.VMEM((1, nodes), jnp.int32),
                pltpu.VMEM((places, locals_, quarter, width), bf16),
                pltpu.VMEM((width, units), bf16),
                pltpu.VMEM((places, rows, units), bf16),
                pltpu.VMEM((rows, units), bf16),
                pltpu.VMEM((places, locals_, variables, quarter), bf16),
                pltpu.VMEM((places, locals_, variables, quarter), bf16),
                pltpu.VMEM((members, variables, quarter), f32),
                pltpu.VMEM((members, variables, quarter), f32),
                pltpu.VMEM((places, locals_, variables, quarter), bf16),
                pltpu.VMEM((places, locals_, variables, quarter), bf16),
                pltpu.VMEM((cells, nodes), bf16),
                pltpu.VMEM((nodes, cells), bf16),
                pltpu.VMEM((nodes, locals_ * LANES), bf16),
                pltpu.VMEM((spaces, CELL_DEV, LANES), bf16),
                pltpu.VMEM((spaces, CELL_DEV, LANES), bf16),
                pltpu.VMEM((spaces, CELL_DEV, locals_ * LANES), bf16),
                pltpu.VMEM((spaces, CELL_DEV, locals_ * LANES), bf16),
                pltpu.VMEM((places, variables, locals_ * CELL_DEV), bf16),
                pltpu.VMEM((CELL_DEV, locals_ * LANES), bf16),
                pltpu.VMEM((spaces, CELL_DEV, locals_ * LANES), bf16),
                pltpu.VMEM((rows, LANES), bf16),
                pltpu.VMEM((places, 8, LANES), f32),
                pltpu.VMEM((spaces, 8, LANES), f32),
                pltpu.SemaphoreType.DMA((places + 1,)),
                pltpu.SemaphoreType.DMA((6,)),
                single, single, single, pltpu.SemaphoreType.DMA((places,)),
            ]
            + [single] * 12,
            compiler_params=pltpu.CompilerParams(
                collective_id=0, has_side_effects=True, vmem_limit_bytes=36 * 2**20
            ),
            name="exchange",
        )(*map(in_hbm, (latent, w_in, b_in[None], w_out.T, b_out[None], target.T, area[None], cell_of[None])))

        latent_grad, scores = pl.pallas_call(
            functools.partial(backward, places, scaling),
            out_shape=(
                jax.ShapeDtypeStruct((locals_, nodes, width), bf16),
                jax.ShapeDtypeStruct((2,), f32),
            ),
            in_specs=[inside] * 4,
            out_specs=(anywhere, anywhere),
            scratch_shapes=[
                pltpu.VMEM((locals_, quarter, width), bf16),
                pltpu.SMEM((2,), f32),
                pltpu.SemaphoreType.DMA((places + width // COLS,)),
            ],
            compiler_params=pltpu.CompilerParams(vmem_limit_bytes=16 * 2**20),
            name="backward",
        )(early, pg, turned, stats)
        return latent_grad, scores

    in_specs = (
        P("member", "space", None),
        P(),
        P(),
        P(),
        P(),
        P("space", None),
        P("space"),
        P("space"),
    )
    out_specs = (P("member", "space", None), P())
    return jax.shard_map(shards, mesh=mesh, in_specs=in_specs, out_specs=out_specs, check_vma=False)
```

time: 38.8 us -> 36.8 us (0.948)
  Pallas kernels: 38 us -> 36 us
    pallas_call x1, Pallas kernels: 35.2 us -> 33.7 us  [shards(): pl.pallas_call(functools.partial(exchange, spaces, places, scaling), out_...]
    pallas_call x1, Pallas kernels: 2.82 us -> 2.37 us  [shards(): pl.pallas_call(functools.partial(backward, places, scaling), out_shape=(j...]
where the time goes in v3:
time: 36.8 us; the launch traced here: 36.7 us
  Pallas kernels  36 us (98%)
  between operations  0.64 us (2%)
    pallas_call x1, Pallas kernels, shards(): pl.pallas_call(functools.partial(exchange, spaces, places, scaling), out_...  33.7 us
    pallas_call x1, Pallas kernels, shards(): pl.pallas_call(functools.partial(backward, places, scaling), out_shape=(j...  2.37 us

profile of v3, /device:TPU:0, one launch (start us, length us, event | category | flops | bytes accessed | tf_op | source)
XLA Modules:
  0.0 36.7 jit_solution(2548573992134589142)
XLA Ops:
  0.6 33.7 %exchange.1 = (bf16[3,4,128,1024]{3,2,1,0:T(8,128)(2,1)S(1)}, bf16[512,1024]{1,0:T(8,128)(2,1)S(1)}, bf16[1024,1024]{1,0:T(8,128)(2,1)S(1)}, f32[8,128]{1,0:T(8,128)S(1)}) custom-call(bf16[4,512,1024]{2,1,0:T(8,128)(2,1)} %latent.1, bf16[1024,1024]{1,0:T(8,128)(2,1)} %w_in.1, f32[1,1024]{1,0:T(1,128)} %bitcast.8, bf16[96,1024]{1,0:T(8,128)(2,1)} %bitcast.6, ...), custom_call_target="tpu_custom_call" | custom-call | tf_op jit(solution)/shard_map/exchange/pallas_call | solution.py:421
  34.3 2.4 %backward.1 = (bf16[4,512,1024]{2,1,0:T(8,128)(2,1)}, f32[2]{0:T(128)}) custom-call(bf16[3,4,128,1024]{3,2,1,0:T(8,128)(2,1)S(1)} %get-tuple-element.6.early, bf16[512,1024]{1,0:T(8,128)(2,1)S(1)} %get-tuple-element.7.pg, bf16[1024,1024]{1,0:T(8,128)(2,1)S(1)} %get-tuple-element.8.turned, f32[8,128]{1,0:T(8,128)S(1)} %get-tuple-element.9.stats), custom_call_target="tpu_custom_call" | custom-call | tf_op jit(solution)/shard_map/backward/pallas_call | solution.py:472

commit v4 on v3

--- a/solution.py
+++ b/solution.py
@@ -36,15 +36,17 @@
              early, pg_out, turned, stats_out,
              b_in, w_out, b_out, target, area, cell_of, lat_buf, w_buf, slope_buf, act,
              psend, precv, p32, grad, gsend, grecv, hot, turned_hot, pcat, qsend, qrecv, csend, crecv,
-             mrecv, dsend, drecv, up_buf, lmem, lspace,
+             zsend, zrecv, mrecv, nrecv, dsend, drecv, up_buf, lmem, lspace,
              load_sem, small_sem, ps_sem, pr_sem, gs_sem, gr_sem, qs_sem, qr_sem, cs_sem, cr_sem,
-             ms_sem, mr_sem, ds_sem, dr_sem, ls_sem, lr_sem, ts_sem, tr_sem):
+             zs_sem, zr_sem, ms_sem, mr_sem, ns_sem, nr_sem, ds_sem, dr_sem, ls_sem, lr_sem, ts_sem, tr_sem):
     ms = lax.axis_index("space")
     mm = lax.axis_index("member")
-    locals_, quarter, width = lat_buf.shape[1:]
+    locals_, nodes, width = lat_buf.shape
+    quarter = nodes // places
     units = w_buf.shape[1]
     variables = target.shape[0]
     members = locals_ * places
+    rows = locals_ * quarter
     cells = CELL_DEV * spaces
     pair_scale = 1.0 / (members * (members - 1))
 
@@ -85,11 +87,10 @@
     def nodes_of(q):
         return pl.ds(pl.multiple_of(q * quarter, quarter), quarter)
 
-    def load_chunk(i):
-        q = lax.rem(mm + 1 + i, places)
-        return pltpu.make_async_copy(latent.at[:, nodes_of(q), :], lat_buf.at[i], load_sem.at[i])
-
-    w_copy = pltpu.make_async_copy(w_in, w_buf, load_sem.at[places])
+    def load_chunk(j):
+        return pltpu.make_async_copy(latent.at[j], lat_buf.at[j], load_sem.at[j])
+
+    w_copy = pltpu.make_async_copy(w_in, w_buf, load_sem.at[locals_])
     small = [
         pltpu.make_async_copy(src, dst, small_sem.at[n])
         for n, (src, dst) in enumerate((
@@ -102,8 +103,8 @@
     load_chunk(0).start()
     for copy in small[3:]:
         copy.start()
-    for i in range(1, places):
-        load_chunk(i).start()
+    for j in range(1, locals_):
+        load_chunk(j).start()
     barrier = pltpu.get_barrier_semaphore()
     for o in range(1, places):
         pl.semaphore_signal(barrier, inc=1, device_id={"member": member_peer(o)}, device_id_type=MESH)
@@ -112,19 +113,21 @@
 
     for copy in small[:3]:
         copy.wait()
-    match = lax.broadcasted_iota(jnp.int32, (cells, cell_of.shape[1]), 0) == cell_of[...]
-    ones = jnp.where(match, 1.0, 0.0)
-    hot[...] = ones.astype(bf16)
-    counts = halves(jnp.sum(ones, axis=1, keepdims=True))
-    areas = halves(jnp.sum(jnp.where(match, area[...], 0.0), axis=1, keepdims=True))
-    whole = halves(jnp.sum(area[...], axis=1, keepdims=True))
     spare = LANES - variables
+    match = lax.broadcasted_iota(jnp.int32, (cells, nodes), 0) == cell_of[...]
+    hot[...] = jnp.where(match, 1.0, 0.0).astype(bf16)
+    row = lax.broadcasted_iota(jnp.int32, (spare, nodes), 0)
     t_high, t_low = halves(target[...])
-    sums = dot_t(hot[...], t_high.astype(bf16)) + dot_t(hot[...], t_low.astype(bf16))
+    a_high, a_low = halves(area[...])
+    firsts = jnp.where(row == 0, 1.0, jnp.where(row == 1, a_high, 0.0))
+    seconds = jnp.where(row == 1, a_low, 0.0)
+    sums = dot_t(hot[...], jnp.concatenate([t_high, firsts], axis=0).astype(bf16))
+    sums = sums + dot_t(hot[...], jnp.concatenate([t_low, seconds], axis=0).astype(bf16))
     lane = lax.broadcasted_iota(jnp.int32, (cells, LANES), 1)
-    meta = jnp.concatenate([sums, jnp.zeros((cells, spare), f32)], axis=1)
-    for n, value in enumerate(counts + areas + whole):
-        meta = jnp.where(lane == variables + n, value, meta)
+    lows = pltpu.roll(halves(sums)[1], 2, 1)
+    meta = jnp.where(lane < variables + 2, sums, lows)
+    for n, value in enumerate(halves(jnp.sum(area[...], axis=1, keepdims=True))):
+        meta = jnp.where(lane == variables + 4 + n, value, meta)
     for s in range(spaces):
         qsend[s] = meta[s * CELL_DEV:(s + 1) * CELL_DEV].astype(bf16)
     w_out[variables:, :] = jnp.zeros((spare, units), bf16)
@@ -133,46 +136,45 @@
         copy.wait()
     w_copy.wait()
 
-    def forward(i, carry):
-        q = lax.rem(mm + 1 + i, places)
-        load_chunk(i).wait()
-
-        rows = lat_buf[i].reshape(locals_ * quarter, width)
-        x = jnp.dot(rows, w_buf[...], preferred_element_type=f32) + b_in[...]
+    def forward(j, carry):
+        load_chunk(j).wait()
+        x = jnp.dot(lat_buf[j], w_buf[...], preferred_element_type=f32) + b_in[...]
         act[...] = (x * (0.5 * jnp.tanh(0.5 * x) + 0.5)).astype(bf16)
-        slope_buf[i] = x.astype(bf16)
+        slope_buf[j] = x.astype(bf16)
         bias = jnp.concatenate([b_out[...], jnp.zeros((1, spare), f32)], axis=1)
         rounded = (dot_t(act[...], w_out[...]) + bias).astype(bf16)
-        for j in range(locals_):
-            block = rounded[j * quarter:(j + 1) * quarter]
-            psend[q, j] = block.astype(f32).T[:variables].astype(bf16)
-            pcat[nodes_of(q), j * LANES:(j + 1) * LANES] = block
-        return carry
-
-    def forward_send(i, carry):
-        forward(i, carry)
-
-        @pl.when(i == 0)
+        pcat[:, pl.ds(pl.multiple_of(j * LANES, LANES), LANES)] = rounded
+        for q in range(places):
+            psend[q, j] = rounded[q * quarter:(q + 1) * quarter].astype(f32).T[:variables].astype(bf16)
+
+        @pl.when(j == 0)
         def _():
             pl.semaphore_wait(barrier, places + spaces - 2)
 
-        to_member(psend.at[member_peer(i + 1)], precv, ps_sem, pr_sem, i + 1).start()
-
-        @pl.when(i == 0)
+        for o in range(1, places):
+            pltpu.make_async_remote_copy(
+                src_ref=psend.at[member_peer(o), j], dst_ref=precv.at[mm, j], send_sem=ps_sem, recv_sem=pr_sem,
+                device_id={"member": member_peer(o)}, device_id_type=MESH).start()
+
+        @pl.when(j == 0)
         def _():
             for o in range(1, spaces):
                 to_space(qsend.at[space_peer(o)], qrecv, qs_sem, qr_sem, o).start()
 
         return carry
 
-    lax.fori_loop(0, places - 1, forward_send, 0)
-    forward(places - 1, 0)
-
-    sums = jnp.dot(hot[...], pcat[...], preferred_element_type=f32).astype(bf16)
-    for s in range(spaces):
-        csend[s] = sums[s * CELL_DEV:(s + 1) * CELL_DEV]
-    for o in range(1, spaces):
-        to_space(csend.at[space_peer(o)], crecv, cs_sem, cr_sem, o).start()
+    def spread(src, dst, ss, rs, lanes):
+        sums = jnp.dot(hot[...], pcat[:, lanes], preferred_element_type=f32).astype(bf16)
+        for s in range(spaces):
+            src[s] = sums[s * CELL_DEV:(s + 1) * CELL_DEV]
+        for o in range(1, spaces):
+            to_space(src.at[space_peer(o)], dst, ss, rs, o).start()
+
+    ahead = (locals_ - 1) * LANES
+    lax.fori_loop(0, locals_ - 1, forward, 0)
+    spread(csend, crecv, cs_sem, cr_sem, slice(0, ahead))
+    forward(locals_ - 1, 0)
+    spread(zsend, zrecv, zs_sem, zr_sem, slice(ahead, ahead + LANES))
 
     def turn(n, carry):
         at = pl.ds(pl.multiple_of(n * COLS, COLS), COLS)
@@ -189,8 +191,8 @@
     meta = qrecv[0].astype(f32)
     for s in range(1, spaces):
         meta = meta + qrecv[s].astype(f32)
-    cell_count = meta[:, variables:variables + 1] + meta[:, variables + 1:variables + 2]
-    cell_area = meta[:, variables + 2:variables + 3] + meta[:, variables + 3:variables + 4]
+    cell_count = meta[:, variables:variables + 1] + meta[:, variables + 2:variables + 3]
+    cell_area = meta[:, variables + 1:variables + 2] + meta[:, variables + 3:variables + 4]
     all_area = meta[0:1, variables + 4:variables + 5] + meta[0:1, variables + 5:variables + 6]
     divisor = jnp.maximum(cell_count, 1.0)
     cell_lane = lax.broadcasted_iota(jnp.int32, (CELL_DEV, LANES), 1)
@@ -201,25 +203,30 @@
     cell_weight = facts[variables + 1:variables + 2]
 
     def slopes(n, carry):
-        i, at = lax.div(n, units // SLIM), pl.ds(pl.multiple_of(lax.rem(n, units // SLIM) * SLIM, SLIM), SLIM)
-        x = slope_buf[i, :, at].astype(f32)
+        j, at = lax.div(n, units // SLIM), pl.ds(pl.multiple_of(lax.rem(n, units // SLIM) * SLIM, SLIM), SLIM)
+        x = slope_buf[j, :, at].astype(f32)
         s = 0.5 * jnp.tanh(0.5 * x) + 0.5
-        slope_buf[i, :, at] = (s + x * s * (1.0 - s)).astype(bf16)
+        slope_buf[j, :, at] = (s + x * s * (1.0 - s)).astype(bf16)
         return carry
 
-    half = places // 2 * (units // SLIM)
+    def average(src, near, far, means_buf, ss, rs):
+        near[ms] = src[ms]
+        far.wait_recv()
+        total = near[0].astype(f32)
+        for s in range(1, spaces):
+            total = total + near[s].astype(f32)
+        means_buf[mm] = (total / divisor).astype(bf16)
+        for o in range(1, places):
+            to_member(means_buf.at[mm], means_buf, ss, rs, o).start()
+
+    average(csend, crecv, all_spaces(crecv, cs_sem, cr_sem), mrecv, ms_sem, mr_sem)
+    half = locals_ // 2 * (units // SLIM)
     lax.fori_loop(0, half, slopes, 0)
-
-    crecv[ms] = csend[ms]
-    all_spaces(crecv, cs_sem, cr_sem).wait_recv()
-    total = crecv[0].astype(f32)
-    for s in range(1, spaces):
-        total = total + crecv[s].astype(f32)
-    means = (total / divisor).astype(bf16).astype(f32)
-    own = jnp.concatenate([means[:, j * LANES:(j + 1) * LANES] for j in range(locals_)], axis=0).T[:variables]
-    mrecv[mm] = own.astype(bf16)
-    for o in range(1, places):
-        to_member(mrecv.at[mm], mrecv, ms_sem, mr_sem, o).start()
+    average(zsend, zrecv, all_spaces(zrecv, zs_sem, zr_sem), nrecv, ns_sem, nr_sem)
+
+    def members_of(place):
+        parts = [mrecv[place, :, j * LANES:(j + 1) * LANES] for j in range(locals_ - 1)] + [nrecv[place]]
+        return jnp.concatenate(parts, axis=0).astype(f32).T[:variables]
 
     precv[mm] = psend[mm]
     truths = target[:, nodes_of(mm)]
@@ -270,16 +277,19 @@
     for j in range(locals_):
         grecv[mm, j] = (grad[mm * locals_ + j] * scale).astype(bf16)
 
-    lax.fori_loop(half, places * (units // SLIM), slopes, 0)
-
+    if places > 2:
+        send_grads(2)
+
+    own = members_of(mm)
     all_members(mrecv, ms_sem, mr_sem).wait_recv()
+    all_members(nrecv, ns_sem, nr_sem).wait_recv()
     d = own - cell_target
     sq = jnp.sum(d * d, axis=0, keepdims=True) * (1.0 / variables) + epsilon
     inv = lax.rsqrt(sq)
     coarse = d * (inv * (1.0 / members))
     coarse_dist = sq * inv * (1.0 / members)
     for o in range(places):
-        theirs = mrecv[member_peer(o)].astype(f32)
+        theirs = members_of(member_peer(o)) if o else own
         for r in range(locals_):
             if o == 0 and r == 0:
                 continue
@@ -301,8 +311,9 @@
     lmem[mm] = jnp.where(row == 0, jnp.sum(fine_loss, axis=1, keepdims=True), coarse_loss)
     for o in range(1, places):
         to_member(lmem.at[mm], lmem, ls_sem, lr_sem, o).start()
-    for o in range(2, places):
+    for o in range(3, places):
         send_grads(o)
+    lax.fori_loop(half, locals_ * (units // SLIM), slopes, 0)
 
     all_spaces(drecv, ds_sem, dr_sem).wait_recv()
     factor = scaling / all_area
@@ -319,7 +330,8 @@
 
     def hidden_to(pg, i):
         h = jnp.dot(up_buf[...], w_out[...], preferred_element_type=f32)
-        pg[...] = (h * slope_buf[i].astype(f32)).astype(bf16)
+        slope = slope_buf[:, nodes_of(lax.rem(mm + 1 + i, places)), :].reshape(rows, units)
+        pg[...] = (h * slope.astype(f32)).astype(bf16)
 
     def finish(i):
         upstream(i)
@@ -355,10 +367,12 @@
 
     all_members(psend, ps_sem, pr_sem).wait_send()
     all_members(mrecv, ms_sem, mr_sem).wait_send()
+    all_members(nrecv, ns_sem, nr_sem).wait_send()
     all_members(gsend, gs_sem, gr_sem.at[mm]).wait_send()
     all_members(lmem, ls_sem, lr_sem).wait_send()
     all_spaces(qsend, qs_sem, qr_sem).wait_send()
     all_spaces(csend, cs_sem, cr_sem).wait_send()
+    all_spaces(zsend, zs_sem, zr_sem).wait_send()
     all_spaces(drecv, ds_sem, dr_sem).wait_send()
     all_spaces(lspace, ts_sem, tr_sem).wait_send()
 
@@ -435,9 +449,9 @@
                 pltpu.VMEM((variables, nodes), f32),
                 pltpu.VMEM((1, nodes), f32),
                 pltpu.VMEM((1, nodes), jnp.int32),
-                pltpu.VMEM((places, locals_, quarter, width), bf16),
+                pltpu.VMEM((locals_, nodes, width), bf16),
                 pltpu.VMEM((width, units), bf16),
-                pltpu.VMEM((places, rows, units), bf16),
+                pltpu.VMEM((locals_, nodes, units), bf16),
                 pltpu.VMEM((rows, units), bf16),
                 pltpu.VMEM((places, locals_, variables, quarter), bf16),
                 pltpu.VMEM((places, locals_, variables, quarter), bf16),
@@ -450,19 +464,22 @@
                 pltpu.VMEM((nodes, locals_ * LANES), bf16),
                 pltpu.VMEM((spaces, CELL_DEV, LANES), bf16),
                 pltpu.VMEM((spaces, CELL_DEV, LANES), bf16),
-                pltpu.VMEM((spaces, CELL_DEV, locals_ * LANES), bf16),
-                pltpu.VMEM((spaces, CELL_DEV, locals_ * LANES), bf16),
-                pltpu.VMEM((places, variables, locals_ * CELL_DEV), bf16),
+                pltpu.VMEM((spaces, CELL_DEV, (locals_ - 1) * LANES), bf16),
+                pltpu.VMEM((spaces, CELL_DEV, (locals_ - 1) * LANES), bf16),
+                pltpu.VMEM((spaces, CELL_DEV, LANES), bf16),
+                pltpu.VMEM((spaces, CELL_DEV, LANES), bf16),
+                pltpu.VMEM((places, CELL_DEV, (locals_ - 1) * LANES), bf16),
+                pltpu.VMEM((places, CELL_DEV, LANES), bf16),
                 pltpu.VMEM((CELL_DEV, locals_ * LANES), bf16),
                 pltpu.VMEM((spaces, CELL_DEV, locals_ * LANES), bf16),
                 pltpu.VMEM((rows, LANES), bf16),
                 pltpu.VMEM((places, 8, LANES), f32),
                 pltpu.VMEM((spaces, 8, LANES), f32),
-                pltpu.SemaphoreType.DMA((places + 1,)),
+                pltpu.SemaphoreType.DMA((locals_ + 1,)),
                 pltpu.SemaphoreType.DMA((6,)),
                 single, single, single, pltpu.SemaphoreType.DMA((places,)),
             ]
-            + [single] * 12,
+            + [single] * 16,
             compiler_params=pltpu.CompilerParams(
                 collective_id=0, has_side_effects=True, vmem_limit_bytes=36 * 2**20
             ),

time: 36.8 us -> 37.4 us (1.016)
  Pallas kernels: 36 us -> 36.6 us
    pallas_call x1, Pallas kernels: 33.7 us -> 34.2 us  [shards(): pl.pallas_call(functools.partial(exchange, spaces, places, scaling), out_...]
where the time goes in v4:
time: 37.4 us; the launch traced here: 37.2 us
  Pallas kernels  36.6 us (98%)
  between operations  0.64 us (2%)
    pallas_call x1, Pallas kernels, shards(): pl.pallas_call(functools.partial(exchange, spaces, places, scaling), out_...  34.2 us
    pallas_call x1, Pallas kernels, shards(): pl.pallas_call(functools.partial(backward, places, scaling), out_shape=(j...  2.37 us

profile of v4, /device:TPU:0, one launch (start us, length us, event | category | flops | bytes accessed | tf_op | source)
XLA Modules:
  0.0 37.2 jit_solution(1563789370613955606)
XLA Ops:
  0.6 34.2 %exchange.1 = (bf16[3,4,128,1024]{3,2,1,0:T(8,128)(2,1)S(1)}, bf16[512,1024]{1,0:T(8,128)(2,1)S(1)}, bf16[1024,1024]{1,0:T(8,128)(2,1)S(1)}, f32[8,128]{1,0:T(8,128)S(1)}) custom-call(bf16[4,512,1024]{2,1,0:T(8,128)(2,1)} %latent.1, bf16[1024,1024]{1,0:T(8,128)(2,1)} %w_in.1, f32[1,1024]{1,0:T(1,128)} %bitcast.8, bf16[96,1024]{1,0:T(8,128)(2,1)} %bitcast.6, ...), custom_call_target="tpu_custom_call" | custom-call | tf_op jit(solution)/shard_map/exchange/pallas_call | solution.py:435
  34.8 2.4 %backward.1 = (bf16[4,512,1024]{2,1,0:T(8,128)(2,1)}, f32[2]{0:T(128)}) custom-call(bf16[3,4,128,1024]{3,2,1,0:T(8,128)(2,1)S(1)} %get-tuple-element.6.early, bf16[512,1024]{1,0:T(8,128)(2,1)S(1)} %get-tuple-element.7.pg, bf16[1024,1024]{1,0:T(8,128)(2,1)S(1)} %get-tuple-element.8.turned, f32[8,128]{1,0:T(8,128)S(1)} %get-tuple-element.9.stats), custom_call_target="tpu_custom_call" | custom-call | tf_op jit(solution)/shard_map/backward/pallas_call | solution.py:489

commit v5 on v4

--- a/solution.py
+++ b/solution.py
@@ -220,8 +220,6 @@
             to_member(means_buf.at[mm], means_buf, ss, rs, o).start()
 
     average(csend, crecv, all_spaces(crecv, cs_sem, cr_sem), mrecv, ms_sem, mr_sem)
-    half = locals_ // 2 * (units // SLIM)
-    lax.fori_loop(0, half, slopes, 0)
     average(zsend, zrecv, all_spaces(zrecv, zs_sem, zr_sem), nrecv, ns_sem, nr_sem)
 
     def members_of(place):
@@ -308,12 +306,12 @@
     coarse_loss = jnp.sum(cell_weight * coarse_dist, axis=1, keepdims=True)
 
     row = lax.broadcasted_iota(jnp.int32, (8, LANES), 0)
-    lmem[mm] = jnp.where(row == 0, jnp.sum(fine_loss, axis=1, keepdims=True), coarse_loss)
-    for o in range(1, places):
-        to_member(lmem.at[mm], lmem, ls_sem, lr_sem, o).start()
+    lspace[ms] = jnp.where(row == 0, jnp.sum(fine_loss, axis=1, keepdims=True), coarse_loss)
+    for o in range(1, spaces):
+        to_space(lspace.at[ms], lspace, ts_sem, tr_sem, o).start()
     for o in range(3, places):
         send_grads(o)
-    lax.fori_loop(half, locals_ * (units // SLIM), slopes, 0)
+    lax.fori_loop(0, locals_ * (units // SLIM), slopes, 0)
 
     all_spaces(drecv, ds_sem, dr_sem).wait_recv()
     factor = scaling / all_area
@@ -339,14 +337,14 @@
         g = jnp.dot(act[...], turned[...], preferred_element_type=f32)
         early[i - 1] = (g * factor).astype(bf16).reshape(locals_, quarter, width)
 
+    all_spaces(lspace, ts_sem, tr_sem).wait_recv()
+    loss = lspace[0]
+    for s in range(1, spaces):
+        loss = loss + lspace[s]
+    lmem[mm] = loss
+    for o in range(1, places):
+        to_member(lmem.at[mm], lmem, ls_sem, lr_sem, o).start()
     finish(places - 1)
-    all_members(lmem, ls_sem, lr_sem).wait_recv()
-    loss = lmem[0]
-    for m in range(1, places):
-        loss = loss + lmem[m]
-    lspace[ms] = loss
-    for o in range(1, spaces):
-        to_space(lspace.at[ms], lspace, ts_sem, tr_sem, o).start()
 
     def arrived(n, carry):
         i = places - 2 - n
@@ -359,10 +357,10 @@
     upstream(0)
     hidden_to(pg_out, 0)
 
-    all_spaces(lspace, ts_sem, tr_sem).wait_recv()
-    loss = lspace[0]
-    for s in range(1, spaces):
-        loss = loss + lspace[s]
+    all_members(lmem, ls_sem, lr_sem).wait_recv()
+    loss = lmem[0]
+    for m in range(1, places):
+        loss = loss + lmem[m]
     stats_out[...] = jnp.where(row == 2, all_area, loss)
 
     all_members(psend, ps_sem, pr_sem).wait_send()

time: 37.4 us -> 36.2 us (0.968)
  Pallas kernels: 36.6 us -> 35.4 us
    pallas_call x1, Pallas kernels: 34.2 us -> 33 us  [shards(): pl.pallas_call(functools.partial(exchange, spaces, places, scaling), out_...]
where the time goes in v5:
time: 36.2 us; the launch traced here: 36 us
  Pallas kernels  35.4 us (98%)
  between operations  0.64 us (2%)
    pallas_call x1, Pallas kernels, shards(): pl.pallas_call(functools.partial(exchange, spaces, places, scaling), out_...  33 us
    pallas_call x1, Pallas kernels, shards(): pl.pallas_call(functools.partial(backward, places, scaling), out_shape=(j...  2.37 us

profile of v5, /device:TPU:0, one launch (start us, length us, event | category | flops | bytes accessed | tf_op | source)
XLA Modules:
  0.0 36.0 jit_solution(720628336793464587)
XLA Ops:
  0.6 33.0 %exchange.1 = (bf16[3,4,128,1024]{3,2,1,0:T(8,128)(2,1)S(1)}, bf16[512,1024]{1,0:T(8,128)(2,1)S(1)}, bf16[1024,1024]{1,0:T(8,128)(2,1)S(1)}, f32[8,128]{1,0:T(8,128)S(1)}) custom-call(bf16[4,512,1024]{2,1,0:T(8,128)(2,1)} %latent.1, bf16[1024,1024]{1,0:T(8,128)(2,1)} %w_in.1, f32[1,1024]{1,0:T(1,128)} %bitcast.8, bf16[96,1024]{1,0:T(8,128)(2,1)} %bitcast.6, ...), custom_call_target="tpu_custom_call" | custom-call | tf_op jit(solution)/shard_map/exchange/pallas_call | solution.py:433
  33.6 2.4 %backward.1 = (bf16[4,512,1024]{2,1,0:T(8,128)(2,1)}, f32[2]{0:T(128)}) custom-call(bf16[3,4,128,1024]{3,2,1,0:T(8,128)(2,1)S(1)} %get-tuple-element.6.early, bf16[512,1024]{1,0:T(8,128)(2,1)S(1)} %get-tuple-element.7.pg, bf16[1024,1024]{1,0:T(8,128)(2,1)S(1)} %get-tuple-element.8.turned, f32[8,128]{1,0:T(8,128)S(1)} %get-tuple-element.9.stats), custom_call_target="tpu_custom_call" | custom-call | tf_op jit(solution)/shard_map/backward/pallas_call | solution.py:487

commit v6 on v5

--- a/solution.py
+++ b/solution.py
@@ -121,8 +121,8 @@
     a_high, a_low = halves(area[...])
     firsts = jnp.where(row == 0, 1.0, jnp.where(row == 1, a_high, 0.0))
     seconds = jnp.where(row == 1, a_low, 0.0)
-    sums = dot_t(hot[...], jnp.concatenate([t_high, firsts], axis=0).astype(bf16))
-    sums = sums + dot_t(hot[...], jnp.concatenate([t_low, seconds], axis=0).astype(bf16))
+    sums = dot_t(hot[...], jnp.concatenate([t_high, firsts, t_low, seconds], axis=0).astype(bf16))
+    sums = sums[:, :LANES] + sums[:, LANES:]
     lane = lax.broadcasted_iota(jnp.int32, (cells, LANES), 1)
     lows = pltpu.roll(halves(sums)[1], 2, 1)
     meta = jnp.where(lane < variables + 2, sums, lows)
@@ -139,8 +139,10 @@
     def forward(j, carry):
         load_chunk(j).wait()
         x = jnp.dot(lat_buf[j], w_buf[...], preferred_element_type=f32) + b_in[...]
-        act[...] = (x * (0.5 * jnp.tanh(0.5 * x) + 0.5)).astype(bf16)
-        slope_buf[j] = x.astype(bf16)
+        x = x.astype(bf16)
+        slope_buf[j] = x
+        x = x * 0.5
+        act[...] = x * jnp.tanh(x) + x
         bias = jnp.concatenate([b_out[...], jnp.zeros((1, spare), f32)], axis=1)
         rounded = (dot_t(act[...], w_out[...]) + bias).astype(bf16)
         pcat[:, pl.ds(pl.multiple_of(j * LANES, LANES), LANES)] = rounded
@@ -337,6 +339,7 @@
         g = jnp.dot(act[...], turned[...], preferred_element_type=f32)
         early[i - 1] = (g * factor).astype(bf16).reshape(locals_, quarter, width)
 
+    finish(places - 1)
     all_spaces(lspace, ts_sem, tr_sem).wait_recv()
     loss = lspace[0]
     for s in range(1, spaces):
@@ -344,7 +347,6 @@
     lmem[mm] = loss
     for o in range(1, places):
         to_member(lmem.at[mm], lmem, ls_sem, lr_sem, o).start()
-    finish(places - 1)
 
     def arrived(n, carry):
         i = places - 2 - n

time: 36.2 us -> 35.1 us (0.970)
  Pallas kernels: 35.4 us -> 34.3 us
    pallas_call x1, Pallas kernels: 33 us -> 31.9 us  [shards(): pl.pallas_call(functools.partial(exchange, spaces, places, scaling), out_...]
where the time goes in v6:
time: 35.1 us; the launch traced here: 34.9 us
  Pallas kernels  34.3 us (98%)
  between operations  0.64 us (2%)
    pallas_call x1, Pallas kernels, shards(): pl.pallas_call(functools.partial(exchange, spaces, places, scaling), out_...  31.9 us
    pallas_call x1, Pallas kernels, shards(): pl.pallas_call(functools.partial(backward, places, scaling), out_shape=(j...  2.37 us

profile of v6, /device:TPU:0, one launch (start us, length us, event | category | flops | bytes accessed | tf_op | source)
XLA Modules:
  0.0 34.9 jit_solution(4627888851964325268)
XLA Ops:
  0.6 31.9 %exchange.1 = (bf16[3,4,128,1024]{3,2,1,0:T(8,128)(2,1)S(1)}, bf16[512,1024]{1,0:T(8,128)(2,1)S(1)}, bf16[1024,1024]{1,0:T(8,128)(2,1)S(1)}, f32[8,128]{1,0:T(8,128)S(1)}) custom-call(bf16[4,512,1024]{2,1,0:T(8,128)(2,1)} %latent.1, bf16[1024,1024]{1,0:T(8,128)(2,1)} %w_in.1, f32[1,1024]{1,0:T(1,128)} %bitcast.8, bf16[96,1024]{1,0:T(8,128)(2,1)} %bitcast.6, ...), custom_call_target="tpu_custom_call" | custom-call | tf_op jit(solution)/shard_map/exchange/pallas_call | solution.py:435
  32.6 2.4 %backward.1 = (bf16[4,512,1024]{2,1,0:T(8,128)(2,1)}, f32[2]{0:T(128)}) custom-call(bf16[3,4,128,1024]{3,2,1,0:T(8,128)(2,1)S(1)} %get-tuple-element.6.early, bf16[512,1024]{1,0:T(8,128)(2,1)S(1)} %get-tuple-element.7.pg, bf16[1024,1024]{1,0:T(8,128)(2,1)S(1)} %get-tuple-element.8.turned, f32[8,128]{1,0:T(8,128)S(1)} %get-tuple-element.9.stats), custom_call_target="tpu_custom_call" | custom-call | tf_op jit(solution)/shard_map/backward/pallas_call | solution.py:489

commit v7 on v6

--- a/solution.py
+++ b/solution.py
@@ -178,16 +178,6 @@
     forward(locals_ - 1, 0)
     spread(zsend, zrecv, zs_sem, zr_sem, slice(ahead, ahead + LANES))
 
-    def turn(n, carry):
-        at = pl.ds(pl.multiple_of(n * COLS, COLS), COLS)
-        turned[:, at] = w_buf[at, :].T
-        return carry
-
-    lax.fori_loop(0, width // COLS, turn, 0)
-    for q in range(places):
-        at = slice(q * quarter, (q + 1) * quarter)
-        turned_hot[at, :] = hot[:, at].astype(f32).T.astype(bf16)
-
     qrecv[ms] = qsend[ms]
     all_spaces(qrecv, qs_sem, qr_sem).wait_recv()
     meta = qrecv[0].astype(f32)
@@ -222,6 +212,16 @@
             to_member(means_buf.at[mm], means_buf, ss, rs, o).start()
 
     average(csend, crecv, all_spaces(crecv, cs_sem, cr_sem), mrecv, ms_sem, mr_sem)
+    def turn(n, carry):
+        at = pl.ds(pl.multiple_of(n * COLS, COLS), COLS)
+        turned[:, at] = w_buf[at, :].T
+        return carry
+
+    lax.fori_loop(0, width // COLS, turn, 0)
+    for q in range(places):
+        at = slice(q * quarter, (q + 1) * quarter)
+        turned_hot[at, :] = hot[:, at].astype(f32).T.astype(bf16)
+
     average(zsend, zrecv, all_spaces(zrecv, zs_sem, zr_sem), nrecv, ns_sem, nr_sem)
 
     def members_of(place):

time: 35.1 us -> 35.1 us (level)
  no operation moved by 1% of the time
where the time goes in v7:
time: 35.1 us; the launch traced here: 34.9 us
  Pallas kernels  34.3 us (98%)
  between operations  0.64 us (2%)
    pallas_call x1, Pallas kernels, shards(): pl.pallas_call(functools.partial(exchange, spaces, places, scaling), out_...  31.9 us
    pallas_call x1, Pallas kernels, shards(): pl.pallas_call(functools.partial(backward, places, scaling), out_shape=(j...  2.37 us

profile of v7, /device:TPU:0, one launch (start us, length us, event | category | flops | bytes accessed | tf_op | source)
XLA Modules:
  0.0 34.9 jit_solution(431356525402122869)
XLA Ops:
  0.6 31.9 %exchange.1 = (bf16[3,4,128,1024]{3,2,1,0:T(8,128)(2,1)S(1)}, bf16[512,1024]{1,0:T(8,128)(2,1)S(1)}, bf16[1024,1024]{1,0:T(8,128)(2,1)S(1)}, f32[8,128]{1,0:T(8,128)S(1)}) custom-call(bf16[4,512,1024]{2,1,0:T(8,128)(2,1)} %latent.1, bf16[1024,1024]{1,0:T(8,128)(2,1)} %w_in.1, f32[1,1024]{1,0:T(1,128)} %bitcast.8, bf16[96,1024]{1,0:T(8,128)(2,1)} %bitcast.6, ...), custom_call_target="tpu_custom_call" | custom-call | tf_op jit(solution)/shard_map/exchange/pallas_call | solution.py:435
  32.6 2.4 %backward.1 = (bf16[4,512,1024]{2,1,0:T(8,128)(2,1)}, f32[2]{0:T(128)}) custom-call(bf16[3,4,128,1024]{3,2,1,0:T(8,128)(2,1)S(1)} %get-tuple-element.6.early, bf16[512,1024]{1,0:T(8,128)(2,1)S(1)} %get-tuple-element.7.pg, bf16[1024,1024]{1,0:T(8,128)(2,1)S(1)} %get-tuple-element.8.turned, f32[8,128]{1,0:T(8,128)S(1)} %get-tuple-element.9.stats), custom_call_target="tpu_custom_call" | custom-call | tf_op jit(solution)/shard_map/backward/pallas_call | solution.py:489

commit v8 on v7

--- a/solution.py
+++ b/solution.py
@@ -201,17 +201,21 @@
         slope_buf[j, :, at] = (s + x * s * (1.0 - s)).astype(bf16)
         return carry
 
-    def average(src, near, far, means_buf, ss, rs):
+    def average(src, near, far, count, rest, means_buf, ss, rs):
         near[ms] = src[ms]
         far.wait_recv()
         total = near[0].astype(f32)
         for s in range(1, spaces):
             total = total + near[s].astype(f32)
-        means_buf[mm] = (total / divisor).astype(bf16)
+        means = (total / divisor).astype(bf16).astype(f32)
+        packed = jnp.concatenate(rest + [means[:, j * LANES:j * LANES + variables] for j in range(count)], axis=1)
+        sent = means_buf.shape[2]
+        means_buf[mm] = packed[:, :sent].astype(bf16)
         for o in range(1, places):
             to_member(means_buf.at[mm], means_buf, ss, rs, o).start()
-
-    average(csend, crecv, all_spaces(crecv, cs_sem, cr_sem), mrecv, ms_sem, mr_sem)
+        return packed[:, sent:] if sent < packed.shape[1] else None
+
+    rest = average(csend, crecv, all_spaces(crecv, cs_sem, cr_sem), locals_ - 1, [], mrecv, ms_sem, mr_sem)
     def turn(n, carry):
         at = pl.ds(pl.multiple_of(n * COLS, COLS), COLS)
         turned[:, at] = w_buf[at, :].T
@@ -222,11 +226,12 @@
         at = slice(q * quarter, (q + 1) * quarter)
         turned_hot[at, :] = hot[:, at].astype(f32).T.astype(bf16)
 
-    average(zsend, zrecv, all_spaces(zrecv, zs_sem, zr_sem), nrecv, ns_sem, nr_sem)
+    average(zsend, zrecv, all_spaces(zrecv, zs_sem, zr_sem), 1, [rest], nrecv, ns_sem, nr_sem)
 
     def members_of(place):
-        parts = [mrecv[place, :, j * LANES:(j + 1) * LANES] for j in range(locals_ - 1)] + [nrecv[place]]
-        return jnp.concatenate(parts, axis=0).astype(f32).T[:variables]
+        packed = jnp.concatenate([mrecv[place].astype(f32), nrecv[place].astype(f32)], axis=1)
+        parts = [packed[:, j * variables:(j + 1) * variables] for j in range(locals_)]
+        return jnp.concatenate(parts, axis=0).T
 
     precv[mm] = psend[mm]
     truths = target[:, nodes_of(mm)]
@@ -431,6 +436,7 @@
         inside = pl.BlockSpec(memory_space=pltpu.VMEM)
         single = pltpu.SemaphoreType.DMA
         rows = locals_ * quarter
+        first = (locals_ - 1) * variables // LANES * LANES
         scaling = loss_scale * (nodes * spaces)
         early, pg, turned, stats = pl.pallas_call(
             functools.partial(exchange, spaces, places, scaling),
@@ -468,8 +474,8 @@
                 pltpu.VMEM((spaces, CELL_DEV, (locals_ - 1) * LANES), bf16),
                 pltpu.VMEM((spaces, CELL_DEV, LANES), bf16),
                 pltpu.VMEM((spaces, CELL_DEV, LANES), bf16),
-                pltpu.VMEM((places, CELL_DEV, (locals_ - 1) * LANES), bf16),
-                pltpu.VMEM((places, CELL_DEV, LANES), bf16),
+                pltpu.VMEM((places, CELL_DEV, first), bf16),
+                pltpu.VMEM((places, CELL_DEV, locals_ * variables - first), bf16),
                 pltpu.VMEM((CELL_DEV, locals_ * LANES), bf16),
                 pltpu.VMEM((spaces, CELL_DEV, locals_ * LANES), bf16),
                 pltpu.VMEM((rows, LANES), bf16),

time: 35.1 us -> 35.1 us (level)
  no operation moved by 1% of the time
where the time goes in v8:
time: 35.1 us; the launch traced here: 34.9 us
  Pallas kernels  34.2 us (97%)
  between operations  0.64 us (2%)
    pallas_call x1, Pallas kernels, shards(): pl.pallas_call(functools.partial(exchange, spaces, places, scaling), out_...  31.9 us
    pallas_call x1, Pallas kernels, shards(): pl.pallas_call(functools.partial(backward, places, scaling), out_shape=(j...  2.37 us

profile of v8, /device:TPU:0, one launch (start us, length us, event | category | flops | bytes accessed | tf_op | source)
XLA Modules:
  0.0 34.9 jit_solution(5838344338848849554)
XLA Ops:
  0.6 31.9 %exchange.1 = (bf16[3,4,128,1024]{3,2,1,0:T(8,128)(2,1)S(1)}, bf16[512,1024]{1,0:T(8,128)(2,1)S(1)}, bf16[1024,1024]{1,0:T(8,128)(2,1)S(1)}, f32[8,128]{1,0:T(8,128)S(1)}) custom-call(bf16[4,512,1024]{2,1,0:T(8,128)(2,1)} %latent.1, bf16[1024,1024]{1,0:T(8,128)(2,1)} %w_in.1, f32[1,1024]{1,0:T(1,128)} %bitcast.8, bf16[96,1024]{1,0:T(8,128)(2,1)} %bitcast.6, ...), custom_call_target="tpu_custom_call" | custom-call | tf_op jit(solution)/shard_map/exchange/pallas_call | solution.py:441
  32.5 2.4 %backward.1 = (bf16[4,512,1024]{2,1,0:T(8,128)(2,1)}, f32[2]{0:T(128)}) custom-call(bf16[3,4,128,1024]{3,2,1,0:T(8,128)(2,1)S(1)} %get-tuple-element.6.early, bf16[512,1024]{1,0:T(8,128)(2,1)S(1)} %get-tuple-element.7.pg, bf16[1024,1024]{1,0:T(8,128)(2,1)S(1)} %get-tuple-element.8.turned, f32[8,128]{1,0:T(8,128)S(1)} %get-tuple-element.9.stats), custom_call_target="tpu_custom_call" | custom-call | tf_op jit(solution)/shard_map/backward/pallas_call | solution.py:495

commit v9 on v7

--- a/solution.py
+++ b/solution.py
@@ -277,8 +277,8 @@
     for j in range(locals_):
         grecv[mm, j] = (grad[mm * locals_ + j] * scale).astype(bf16)
 
-    if places > 2:
-        send_grads(2)
+    for o in range(2, places):
+        send_grads(o)
 
     own = members_of(mm)
     all_members(mrecv, ms_sem, mr_sem).wait_recv()
@@ -311,8 +311,6 @@
     lspace[ms] = jnp.where(row == 0, jnp.sum(fine_loss, axis=1, keepdims=True), coarse_loss)
     for o in range(1, spaces):
         to_space(lspace.at[ms], lspace, ts_sem, tr_sem, o).start()
-    for o in range(3, places):
-        send_grads(o)
     lax.fori_loop(0, locals_ * (units // SLIM), slopes, 0)
 
     all_spaces(drecv, ds_sem, dr_sem).wait_recv()

time: 35.1 us -> 35.1 us (level)
  no operation moved by 1% of the time
where the time goes in v9:
time: 35.1 us; the launch traced here: 34.9 us
  Pallas kernels  34.3 us (98%)
  between operations  0.64 us (2%)
    pallas_call x1, Pallas kernels, shards(): pl.pallas_call(functools.partial(exchange, spaces, places, scaling), out_...  31.9 us
    pallas_call x1, Pallas kernels, shards(): pl.pallas_call(functools.partial(backward, places, scaling), out_shape=(j...  2.37 us

profile of v9, /device:TPU:0, one launch (start us, length us, event | category | flops | bytes accessed | tf_op | source)
XLA Modules:
  0.0 34.9 jit_solution(12475901549455813619)
XLA Ops:
  0.6 31.9 %exchange.1 = (bf16[3,4,128,1024]{3,2,1,0:T(8,128)(2,1)S(1)}, bf16[512,1024]{1,0:T(8,128)(2,1)S(1)}, bf16[1024,1024]{1,0:T(8,128)(2,1)S(1)}, f32[8,128]{1,0:T(8,128)S(1)}) custom-call(bf16[4,512,1024]{2,1,0:T(8,128)(2,1)} %latent.1, bf16[1024,1024]{1,0:T(8,128)(2,1)} %w_in.1, f32[1,1024]{1,0:T(1,128)} %bitcast.8, bf16[96,1024]{1,0:T(8,128)(2,1)} %bitcast.6, ...), custom_call_target="tpu_custom_call" | custom-call | tf_op jit(solution)/shard_map/exchange/pallas_call | solution.py:433
  32.6 2.4 %backward.1 = (bf16[4,512,1024]{2,1,0:T(8,128)(2,1)}, f32[2]{0:T(128)}) custom-call(bf16[3,4,128,1024]{3,2,1,0:T(8,128)(2,1)S(1)} %get-tuple-element.6.early, bf16[512,1024]{1,0:T(8,128)(2,1)S(1)} %get-tuple-element.7.pg, bf16[1024,1024]{1,0:T(8,128)(2,1)S(1)} %get-tuple-element.8.turned, f32[8,128]{1,0:T(8,128)S(1)} %get-tuple-element.9.stats), custom_call_target="tpu_custom_call" | custom-call | tf_op jit(solution)/shard_map/backward/pallas_call | solution.py:487
